TPU v7x, 256 devices: a whole 4x4x8 slice. The times are simulated.
256 devices in a mesh: row: 8 (over y, x_lo), col: 32 (over z, x_hi, core).
Axes of the slice: x: 4 (x_hi: 2, x_lo: 2; x = x_hi * 2 + x_lo), y: 4, z: 8, core: 2. Of those that a mesh axis runs over, the one named last changes fastest.
Arguments:
- pair_rep: bfloat16 [1024, 1024, 128], P('row', 'col'), may hold values from -6 to 6
- proj_weight: bfloat16 [2, 4, 128, 128], replicated, may hold values from -0.5 to 0.5
- gate_weight: bfloat16 [2, 128, 128], replicated, may hold values from -0.5 to 0.5
- out_weight: bfloat16 [2, 128, 128], replicated, may hold values from -0.5 to 0.5
- in_gain: float32 [2, 128], replicated, may hold values from 0.1 to 1.9
- out_gain: float32 [2, 128], replicated, may hold values from 0.1 to 1.9
Outputs:
- updated_pair: bfloat16 [1024, 1024, 128], P('row', 'col')
All inputs are finite; a program needn't handle non-finite values.
Results may differ from a plain program's by a relative error of at most 0.011.
Values may be sent and summed in bfloat16 or wider, within the bound.
A program may use at most 64 MiB of HBM per device.

v0:
```python
import jax
import jax.numpy as jnp
from jax import lax
from jax.sharding import Mesh
from jax.sharding import PartitionSpec as P

ROW = ("row_0", "row_1")


epsilon = 1e-05


def sum_by_axis(terms, axes):
    subtotal = terms.astype(jnp.bfloat16)
    for axis in axes:
        subtotal = lax.psum_scatter(subtotal, axis, scatter_dimension=0, tiled=True)
    return subtotal.astype(jnp.float32)


def layer_norm(values, gain_row, reduce_axis):
    center = values - jnp.mean(values, axis=reduce_axis, keepdims=True)
    spread = jnp.mean(center * center, axis=reduce_axis, keepdims=True)
    return center * lax.rsqrt(spread + epsilon) * gain_row


def local(pair_rep, proj_weight, gate_weight, out_weight, in_gain, out_gain):
    current = pair_rep
    for update_index in range(2):
        widened = current.astype(jnp.float32)
        normed = layer_norm(widened, in_gain[update_index], 2).astype(jnp.bfloat16)
        projected = jnp.einsum(
            "ijc,pch->phij", normed, proj_weight[update_index], preferred_element_type=jnp.float32
        )
        left_hand = (jax.nn.sigmoid(projected[0]) * projected[1]).astype(jnp.bfloat16)
        right_hand = (jax.nn.sigmoid(projected[2]) * projected[3]).astype(jnp.bfloat16)
        gating = jax.nn.sigmoid(
            jnp.dot(normed, gate_weight[update_index], preferred_element_type=jnp.float32)
        )
        left_rows, right_rows = (
            lax.all_to_all(left_hand, "col", split_axis=0, concat_axis=2, tiled=True),
            lax.all_to_all(right_hand, "col", split_axis=0, concat_axis=2, tiled=True),
        )
        if update_index == 0:
            triangle = jnp.einsum(
                "gik,gjk->igj",
                left_rows,
                lax.all_gather(right_rows, ROW, axis=1, tiled=True),
                preferred_element_type=jnp.float32,
            )
        else:
            triangle = sum_by_axis(
                jnp.einsum(
                    "gki,gkj->igj", left_rows, right_rows, preferred_element_type=jnp.float32
                ),
                ROW,
            )
        returned = lax.all_to_all(
            triangle.astype(jnp.bfloat16), "col", split_axis=2, concat_axis=1, tiled=True
        )
        mixed_rows = layer_norm(
            returned.astype(jnp.float32), out_gain[update_index][None, :, None], 1
        ).astype(jnp.bfloat16)
        update = jnp.einsum(
            "ihj,hc->ijc", mixed_rows, out_weight[update_index], preferred_element_type=jnp.float32
        )
        current = (widened + gating * update).astype(jnp.bfloat16)
    return current


def solution(mesh):
    finer = Mesh(mesh.devices.reshape(4, 2, mesh.shape["col"]), ("row_0", "row_1", "col"))
    placed = (P(ROW, "col", None), P(), P(), P(), P(), P())
    return jax.shard_map(
        local, mesh=finer, in_specs=placed, out_specs=P(ROW, "col", None), check_vma=False
    )
```

profile of v0, /device:TPU:1, one launch (start us, length us, event | category | flops | bytes accessed | tf_op | source)
XLA Modules:
  0.0 535.4 jit_solution(13058157798516220307)
XLA Ops:
  6.5 2.0 copy.75
  9.1 1.4 convolution_bitcast_fusion.1
  10.5 1.1 fusion.49
  11.6 1.7 copy.79
  13.3 40.6 %all_to_all.90 = bf16[128,128,32]{1,2,0:T(8,128)(2,1)S(1)} all-to-all(bf16[128,128,32]{1,2,0:T(8,128)(2,1)} %copy.79), channel_id=1, replica_groups=mesh['row_0'=4,'row_1'=2,'col'=32] {'col'}, dimensions={0} | all-to-all | bytes 2097152 | tf_op jit(solution)/shard_map/all_to_all | solution.py:41
  54.1 1.3 copy.81
  56.4 33.7 %all_to_all.91 = bf16[128,128,32]{1,2,0:T(8,128)(2,1)S(1)} all-to-all(bf16[128,128,32]{1,2,0:T(8,128)(2,1)S(1)} %copy.82), channel_id=1, replica_groups=mesh['row_0'=4,'row_1'=2,'col'=32] {'col'}, dimensions={0} | all-to-all | bytes 2097152 | tf_op jit(solution)/shard_map/all_to_all | solution.py:40
  90.2 142.6 %all-gather.2.cloned.1.call-done = bf16[4,1024,1024]{2,1,0:T(8,128)(2,1)} async-done(((bf16[4,128,1024]{2,1,0:T(8,128)(2,1)}), bf16[4,1024,1024]{2,1,0:T(8,128)(2,1)}) %all-gather.2.cloned.1.call-update) | async-done | bytes 8388624 | tf_op jit(solution)/shard_map/all_gather | solution.py:47
  232.7 5.7 %fusion.42 = bf16[128,4,1024]{0,2,1:T(8,128)(2,1)S(1)} fusion(bf16[4,1024,1024]{2,1,0:T(8,128)(2,1)} %all-gather.2.cloned.1.call-done, bf16[4,128,1024]{1,2,0:T(8,128)(2,1)S(1)} %bitcast.134), kind=kOutput, calls=%fused_computation.62 | convolution fusion | flops 1074266112 | bytes 10485760 | tf_op jit(solution)/shard_map/gik,gjk->igj/dot_general | solution.py:44
  238.5 1.8 copy.85
  240.2 10.4 %all-to-all-start.2 = ((bf16[128,4,1024]{0,1,2:T(4,128)(2,1)}), bf16[128,4,1024]{0,1,2:T(4,128)(2,1)S(1)}, u32[]{:S(2)}, u32[]{:S(2)}) async-start(bf16[128,4,1024]{0,1,2:T(4,128)(2,1)} %copy.85), calls=%async_computation.2 | async-start | bytes 2097152 | tf_op jit(solution)/shard_map/all_to_all | solution.py:57
  250.9 27.6 %all-to-all-done.2 = bf16[128,4,1024]{0,1,2:T(4,128)(2,1)S(1)} async-done(((bf16[128,4,1024]{0,1,2:T(4,128)(2,1)}), bf16[128,4,1024]{0,1,2:T(4,128)(2,1)S(1)}, u32[]{:S(2)}, u32[]{:S(2)}) %all-to-all-start.2) | async-done | bytes 1048608 | tf_op jit(solution)/shard_map/all_to_all | solution.py:57
  280.5 1.2 convert_reduce_fusion
  282.1 1.4 convolution_bitcast_fusion
  283.5 1.1 fusion.51
  284.6 1.7 copy.94
  286.3 6.0 %all-to-all-start.3 = ((bf16[128,128,32]{1,2,0:T(8,128)(2,1)}), bf16[128,128,32]{1,2,0:T(8,128)(2,1)S(1)}, u32[]{:S(2)}, u32[]{:S(2)}) async-start(bf16[128,128,32]{1,2,0:T(8,128)(2,1)} %copy.94), calls=%async_computation.3 | async-start | bytes 2097152 | tf_op jit(solution)/shard_map/all_to_all | solution.py:41
  292.3 1.7 copy.96
  294.0 26.4 %all-to-all-done.3 = bf16[128,128,32]{1,2,0:T(8,128)(2,1)S(1)} async-done(((bf16[128,128,32]{1,2,0:T(8,128)(2,1)}), bf16[128,128,32]{1,2,0:T(8,128)(2,1)S(1)}, u32[]{:S(2)}, u32[]{:S(2)}) %all-to-all-start.3) | async-done | bytes 1048608 | tf_op jit(solution)/shard_map/all_to_all | solution.py:41
  320.4 5.9 %all-to-all-start.4 = ((bf16[128,128,32]{1,2,0:T(8,128)(2,1)}), bf16[128,128,32]{1,2,0:T(8,128)(2,1)}, u32[]{:S(2)}, u32[]{:S(2)}) async-start(bf16[128,128,32]{1,2,0:T(8,128)(2,1)} %copy.96), calls=%async_computation.4 | async-start | bytes 2097152 | tf_op jit(solution)/shard_map/all_to_all | solution.py:40
  326.4 28.0 %all-to-all-done.4 = bf16[128,128,32]{1,2,0:T(8,128)(2,1)} async-done(((bf16[128,128,32]{1,2,0:T(8,128)(2,1)}), bf16[128,128,32]{1,2,0:T(8,128)(2,1)}, u32[]{:S(2)}, u32[]{:S(2)}) %all-to-all-start.4) | async-done | bytes 1048608 | tf_op jit(solution)/shard_map/all_to_all | solution.py:40
  354.4 1.3 copy.97
  355.7 5.6 %convert_bitcast_fusion = bf16[1024,4,1024]{0,2,1:T(8,128)(2,1)} fusion(bf16[4,128,1024]{1,2,0:T(8,128)(2,1)S(1)} %bitcast.125, bf16[4,128,1024]{1,2,0:T(8,128)(2,1)S(1)} %bitcast.126), kind=kOutput, calls=%fused_computation | convolution fusion | flops 1077936128 | bytes 10485760 | tf_op jit(solution)/shard_map/gki,gkj->igj/dot_general | solution.py:52
  361.4 80.3 %reduce-scatter.5.cloned.1.call-done = bf16[256,4,1024]{0,2,1:T(8,128)(2,1)} async-done(((bf16[1024,4,1024]{0,2,1:T(8,128)(2,1)}), bf16[256,4,1024]{0,2,1:T(8,128)(2,1)}) %reduce-scatter.5.cloned.1.call-update) | async-done | bytes 2097168 | tf_op jit(solution)/shard_map/reduce_scatter | solution.py:16
  441.6 4.1 copy.120
  445.8 36.8 %reduce-scatter.7.cloned.1.call-done = bf16[128,4096]{1,0:T(8,128)(2,1)} async-done(((bf16[256,4096]{1,0:T(8,128)(2,1)}), bf16[128,4096]{1,0:T(8,128)(2,1)}) %reduce-scatter.7.cloned.1.call-update) | async-done | bytes 1048592
  482.6 1.6 copy.121
  484.2 1.8 copy.99
  486.0 10.1 %all-to-all-start.5 = ((bf16[128,4,1024]{0,1,2:T(4,128)(2,1)}), bf16[128,4,1024]{0,1,2:T(4,128)(2,1)S(1)}, u32[]{:S(2)}, u32[]{:S(2)}) async-start(bf16[128,4,1024]{0,1,2:T(4,128)(2,1)} %copy.99), calls=%async_computation.6 | async-start | bytes 2097152 | tf_op jit(solution)/shard_map/all_to_all | solution.py:57
  496.3 1.9 fusion.55
  498.2 25.8 %all-to-all-done.5 = bf16[128,4,1024]{0,1,2:T(4,128)(2,1)S(1)} async-done(((bf16[128,4,1024]{0,1,2:T(4,128)(2,1)}), bf16[128,4,1024]{0,1,2:T(4,128)(2,1)S(1)}, u32[]{:S(2)}, u32[]{:S(2)}) %all-to-all-start.5) | async-done | bytes 1048608 | tf_op jit(solution)/shard_map/all_to_all | solution.py:57
  527.2 1.7 copy.105
  (53 shorter events, 7.9 us)
Async XLA Ops:
  6.5 2.6 copy-start.5
  6.5 2.6 copy-start.1
  6.5 226.2 %all-gather.2.cloned.1.call-start = ((), (), s32[]{:S(2)}) async-start(), calls=%async_computation.8 | async-start | bytes 9437184 | tf_op jit(solution)/shard_map/all_gather | solution.py:47
  238.5 12.2 %copy-start.6 = (f32[2,128]{1,0:T(2,128)S(1)}, f32[2,128]{1,0:T(2,128)}, u32[]{:S(2)}) copy-start(f32[2,128]{1,0:T(2,128)} %param.11) | copy-start | bytes 3076
  240.2 38.3 %all-to-all-start.2 = ((bf16[128,4,1024]{0,1,2:T(4,128)(2,1)}), bf16[128,4,1024]{0,1,2:T(4,128)(2,1)S(1)}, u32[]{:S(2)}, u32[]{:S(2)}) async-start(bf16[128,4,1024]{0,1,2:T(4,128)(2,1)} %copy.85), calls=%async_computation.2 | async-start | bytes 2097152 | tf_op jit(solution)/shard_map/all_to_all | solution.py:57
  279.2 0.8 copy-start.3
  279.7 0.9 copy-start.2
  286.3 34.1 %all-to-all-start.3 = ((bf16[128,128,32]{1,2,0:T(8,128)(2,1)}), bf16[128,128,32]{1,2,0:T(8,128)(2,1)S(1)}, u32[]{:S(2)}, u32[]{:S(2)}) async-start(bf16[128,128,32]{1,2,0:T(8,128)(2,1)} %copy.94), calls=%async_computation.3 | async-start | bytes 2097152 | tf_op jit(solution)/shard_map/all_to_all | solution.py:41
  320.4 34.0 %all-to-all-start.4 = ((bf16[128,128,32]{1,2,0:T(8,128)(2,1)}), bf16[128,128,32]{1,2,0:T(8,128)(2,1)}, u32[]{:S(2)}, u32[]{:S(2)}) async-start(bf16[128,128,32]{1,2,0:T(8,128)(2,1)} %copy.96), calls=%async_computation.4 | async-start | bytes 2097152 | tf_op jit(solution)/shard_map/all_to_all | solution.py:40
  326.3 115.4 %reduce-scatter.5.cloned.1.call-start = ((), (), s32[]{:S(2)}) async-start(), calls=%async_computation.9 | async-start | bytes 10485760 | tf_op jit(solution)/shard_map/reduce_scatter | solution.py:16
  361.3 121.3 %reduce-scatter.7.cloned.1.call-start = ((), (), s32[]{:S(2)}) async-start(), calls=%async_computation.10 | async-start | bytes 3145728
  486.0 38.0 %all-to-all-start.5 = ((bf16[128,4,1024]{0,1,2:T(4,128)(2,1)}), bf16[128,4,1024]{0,1,2:T(4,128)(2,1)S(1)}, u32[]{:S(2)}, u32[]{:S(2)}) async-start(bf16[128,4,1024]{0,1,2:T(4,128)(2,1)} %copy.99), calls=%async_computation.6 | async-start | bytes 2097152 | tf_op jit(solution)/shard_map/all_to_all | solution.py:57
  524.6 1.6 copy-start
  524.6 1.6 copy-start.4
Sparse Core Ops, SparseCore 0:
  55.5 177.1 all-gather.1
  361.4 80.1 reduce-scatter.4
  445.9 36.6 reduce-scatter.6
where the time goes:
time: 536 us; the launch traced here: 535 us
  waiting for transfers between devices  367 us (68%)
  blocking collectives  74.3 us (14%)
  starting transfers between devices  32.5 us (6%)
  local copies, waits for them, and re-layouts  24.2 us (5%)
  matrix products  18.5 us (3%)
  between operations  13.4 us (2%)
    all_gather x1, waiting for transfers between devices, local(): lax.all_gather(right_rows, ROW, axis=1, tiled=True)  143 us
    reduce_scatter x1, waiting for transfers between devices, sum_by_axis(): subtotal = lax.psum_scatter(subtotal, axis, scatter_dimension=0, tiled=True)  80.3 us
    all_to_all x2, waiting for transfers between devices, local(): lax.all_to_all(triangle.astype(jnp.bfloat16), 'col', split_axis=2, concat...  53.4 us
    all_to_all x1, blocking collectives, local(): lax.all_to_all(right_hand, 'col', split_axis=0, concat_axis=2, tiled=True)  40.6 us
    unnamed x4, waiting for transfers between devices  36.8 us
    all_to_all x1, blocking collectives, local(): lax.all_to_all(left_hand, 'col', split_axis=0, concat_axis=2, tiled=True)  33.7 us
    all_to_all x1, waiting for transfers between devices, local(): lax.all_to_all(left_hand, 'col', split_axis=0, concat_axis=2, tiled=True)  28 us
    all_to_all x1, waiting for transfers between devices, local(): lax.all_to_all(right_hand, 'col', split_axis=0, concat_axis=2, tiled=True)  26.4 us
  transfers between devices with their start and end apart: 7, of which 7 were waited for; matrix products, arithmetic and copies ran while one was open for 1% of the time, Pallas kernels for 0%

commit v1 on v0

v1 whole, which is shorter than its diff:
```python
import functools

import jax
import jax.numpy as jnp
from jax import lax
from jax.experimental import pallas as pl
from jax.experimental.pallas import tpu as pltpu
from jax.sharding import PartitionSpec as P

EPS = 1e-05
MESH = pl.DeviceIdType.MESH
BF = jnp.bfloat16
F32 = jnp.float32
PITCH = 40
LANES = 512

STAGES = (
    "lz", "ly", "lx", "rx", "ry", "rz", "swap", "az", "ax", "ay", "bx", "by", "bz",
)


def scratch_of(update):
    whole, half = (32, 128), (16, 128)
    target = (2, 2, 8, 2, 2) if update == 0 else (4, 2, 4, 2, 2)
    return {
        "al": (8, 4, 4) + whole,
        "l1": (8, 4, 4) + whole,
        "l2": (4, 8, 4) + whole,
        "dl": target + whole,
        "ar": (8, 4, 4) + whole,
        "r1": (2, 2, 8, 4) + whole,
        "r2": (4, 2, 2, 8) + whole,
        "dr": (2, 2, 8, 2, 2) + whole,
        "ds": (2, 2, 8, 2, 2) + whole,
        "ta": (2, 2, 8, 2, 2) + half,
        "tb": (2, 2, 8, 2, 2) + half,
        "a1": (8, 2, 2, 2, 2) + half,
        "a2": (8, 4, 4) + half,
        "fa": (8, 4, 4) + half,
        "b1": (4, 4, 8) + half,
        "b2": (4, 4, 8) + half,
        "fb": (8, 4, 4) + half,
    }


NAMES = tuple(scratch_of(0))


def kernel(x_ref, pw_ref, gw_ref, ow_ref, ig_ref, og_ref, out_ref, *scratch):
    count = len(NAMES)
    buffers = [dict(zip(NAMES, scratch[u * count : (u + 1) * count])) for u in range(2)]
    wt, norm, gate, state, stage, right_t, acc, dummy, send_sem, recv_sem = scratch[2 * count :]

    row, col = lax.axis_index("row"), lax.axis_index("col")
    y, xl = lax.div(row, 2), lax.rem(row, 2)
    z, xh, core = lax.div(col, 4), lax.rem(lax.div(col, 2), 2), lax.rem(col, 2)
    x = xh * 2 + xl
    other = 1 - core

    def device(tx, ty, tz, tc):
        return (ty * 2 + lax.rem(tx, 2), tz * 4 + lax.div(tx, 2) * 2 + tc)

    def turned(own, by, size):
        return lax.rem(own + by, size)

    steps_z, steps_4 = (1, 7, 2, 6, 3, 5, 4), (1, 3, 2)

    barrier = pltpu.get_barrier_semaphore()
    peers = [device(x, y, z, other)]
    for t in (core, other):
        peers += [device(x, y, turned(z, d, 8), t) for d in steps_z]
        peers += [device(x, turned(y, d, 4), z, t) for d in steps_4]
        peers += [device(turned(x, d, 4), y, z, t) for d in steps_4]
    for peer in peers:
        pl.semaphore_signal(barrier, inc=1, device_id=peer, device_id_type=MESH)

    def send(update, name, src, dst, target):
        index = update * len(STAGES) + STAGES.index(name)
        pltpu.make_async_remote_copy(
            src_ref=src,
            dst_ref=dst,
            send_sem=send_sem.at[index],
            recv_sem=recv_sem.at[index],
            device_id=target,
            device_id_type=MESH,
        ).start()

    moved = dict(
        lz=112, ly=96, lx=112, rx=96, ry=96, rz=120, swap=128,
        az=56, ax=56, ay=48, bx=56, by=48, bz=56,
    )

    def descriptor(update, name):
        index = update * len(STAGES) + STAGES.index(name)
        whole = dummy.at[pl.ds(0, moved[name])]
        return pltpu.make_async_remote_copy(
            src_ref=whole,
            dst_ref=whole,
            send_sem=send_sem.at[index],
            recv_sem=recv_sem.at[index],
            device_id=device(x, y, z, other),
            device_id_type=MESH,
        )

    def arrived(update, name):
        descriptor(update, name).wait_recv()

    for u in range(2):
        for p in range(4):
            wt[u, p] = pw_ref[u, p].astype(F32).T.astype(BF)
        wt[u, 4] = gw_ref[u].astype(F32).T.astype(BF)
        wt[u, 5] = ow_ref[u].astype(F32).T.astype(BF)

    chunks = 4096 // LANES
    tiles = LANES // 128

    def lanes(step):
        return pl.ds(pl.multiple_of(step * LANES, LANES), LANES)

    def normalise(update, source):
        gain = jnp.broadcast_to(ig_ref[update : update + 1, :], (128, 128)).T
        gain = jnp.concatenate([gain] * tiles, axis=1)

        @pl.loop(0, chunks)
        def _(step):
            wide = source[:, lanes(step)].astype(F32)
            center = wide - jnp.mean(wide, axis=0, keepdims=True)
            spread = jnp.mean(center * center, axis=0, keepdims=True)
            norm[:, lanes(step)] = (center * lax.rsqrt(spread + EPS) * gain).astype(BF)

    def project(update, first, target):
        weight_gate, weight_value = wt[update, first], wt[update, first + 1]

        @pl.loop(0, chunks)
        def _(step):
            normed = norm[:, lanes(step)]
            opening = jnp.dot(weight_gate, normed, preferred_element_type=F32)
            value = jnp.dot(weight_value, normed, preferred_element_type=F32)
            hand = jax.nn.sigmoid(opening) * value
            for t in range(tiles):
                stage[pl.ds(step * tiles + t, 128, stride=PITCH), :] = hand[:, t * 128 : (t + 1) * 128]

        @pl.loop(0, 8)
        def _(hz):
            for hy in range(4):
                for hx in range(4):
                    start = pl.multiple_of(hz * 16 * PITCH + (hy * 4 + hx) * PITCH, 8)
                    target[hz, hy, hx] = stage[pl.ds(start, 32), :].astype(BF)

    def gates(update):
        weight = wt[update, 4]

        @pl.loop(0, chunks)
        def _(step):
            opening = jnp.dot(weight, norm[:, lanes(step)], preferred_element_type=F32)
            gate[:, lanes(step)] = jax.nn.sigmoid(opening)

    def contract_outgoing(b, half, right):
        left = b["dl"]
        for jb in range(4):
            block = right[jb // 2, jb % 2].reshape(1024, 128)
            right_t[pl.ds(jb * 128, 128), :] = block.T
        for yq in range(2):
            operand = jnp.concatenate(
                [left[yq, lo].reshape(1024, 128) for lo in range(2)], axis=1
            )
            product = jnp.dot(right_t[...], operand, preferred_element_type=F32).astype(BF)
            product = product.reshape(4, 2, 2, 2, 16, 256)
            for lo in range(2):
                piece = product[..., lo * 128 : (lo + 1) * 128]
                b["ta"][yq, lo, pl.ds(half * 4, 4)] = piece[:, :, :, 0]
                b["tb"][yq, lo, pl.ds(half * 4, 4)] = piece[:, :, :, 1]

    def contract_incoming(b, half, right, last):
        left = b["dl"]
        operand = jnp.concatenate(
            [left[half * 2 + kb // 2, kb % 2].reshape(512, 128) for kb in range(4)], axis=1
        )
        for part in range(4):
            zs = slice(part * 2, part * 2 + 2)
            rows = jnp.concatenate(
                [right[kb // 2, kb % 2, zs].reshape(256, 128) for kb in range(4)], axis=1
            )
            product = lax.dot_general(
                rows, operand, (((1,), (1,)), ((), ())), preferred_element_type=F32
            )
            here = slice(part * 256, part * 256 + 256)
            if not last:
                acc[here, :] = product
                continue
            total = (acc[here, :] + product).astype(BF).reshape(2, 2, 2, 2, 16, 512)
            for yq in range(2):
                for lo in range(2):
                    first = (yq * 2 + lo) * 128
                    piece = total[..., first : first + 128]
                    b["ta"][yq, lo, zs] = piece[:, :, :, 0]
                    b["tb"][yq, lo, zs] = piece[:, :, :, 1]

    def finish(update, source, j_half, old, new):
        def total(read):
            def add(hz, running):
                for hy in range(4):
                    for hx in range(4):
                        running = running + read(hz, hy, hx)
                return running

            return lax.fori_loop(0, 8, add, jnp.zeros((16, 128), F32))

        mean = total(lambda *h: source[h].astype(F32)) * (1.0 / 128)

        def square(*h):
            center = source[h].astype(F32) - mean
            return center * center

        inverse = lax.rsqrt(total(square) * (1.0 / 128) + EPS)

        @pl.loop(0, 8)
        def _(hz):
            for hy in range(4):
                for hx in range(4):
                    channel = hz * 16 + hy * 4 + hx
                    mixed = (source[hz, hy, hx].astype(F32) - mean) * inverse * og_ref[update, channel]
                    stage[pl.ds(pl.multiple_of(channel * PITCH, 8), 16), :] = mixed

        weight = wt[update, 5]

        for step in range(16 // tiles):
            mixed = jnp.concatenate(
                [stage[pl.ds(step * tiles + t, 128, stride=PITCH), :] for t in range(tiles)], axis=1
            ).astype(BF)
            change = jnp.dot(weight, mixed, preferred_element_type=F32)
            here = pl.ds(j_half * 2048 + step * LANES, LANES)
            new[:, here] = (old[:, here].astype(F32) + gate[:, here] * change).astype(BF)

    for u in range(2):
        b = buffers[u]
        old, new = (x_ref, state) if u == 0 else (state, out_ref)
        normalise(u, old)
        project(u, 0, b["al"])
        if u == 0:
            pl.semaphore_wait(barrier, len(peers))
        for d in steps_z:
            tz = turned(z, d, 8)
            send(u, "lz", b["al"].at[tz], b["l1"].at[z], device(x, y, tz, core))
        b["l1"][z] = b["al"][z]
        project(u, 2, b["ar"])
        for d in steps_4:
            tx = turned(x, d, 4)
            send(u, "rx", b["ar"].at[:, :, tx], b["r1"].at[xl, xh], device(tx, y, z, core))
        b["r1"][xl, xh] = b["ar"][:, :, x]
        gates(u)

        arrived(u, "rx")
        for d in steps_4:
            ty = turned(y, d, 4)
            send(u, "ry", b["r1"].at[:, :, :, ty], b["r2"].at[y], device(x, ty, z, core))
        b["r2"][y] = b["r1"][:, :, :, y]

        arrived(u, "lz")
        for d in steps_4:
            ty = turned(y, d, 4)
            send(u, "ly", b["l1"].at[:, ty], b["l2"].at[y], device(x, ty, z, core))
        b["l2"][y] = b["l1"][:, y]

        arrived(u, "ry")
        for d in steps_z:
            for t in (core, other):
                tz = turned(z, d, 8)
                send(
                    u, "rz", b["r2"].at[pl.ds(t * 2, 2), :, :, tz],
                    b["dr"].at[:, :, z, :, core], device(x, y, tz, t),
                )
        send(
            u, "rz", b["r2"].at[pl.ds(other * 2, 2), :, :, z],
            b["dr"].at[:, :, z, :, core], device(x, y, z, other),
        )
        b["dr"][:, :, z, :, core] = b["r2"][pl.ds(core * 2, 2), :, :, z]

        arrived(u, "ly")

        def left_of(t, tx):
            if u == 0:
                return b["l2"].at[pl.ds(t * 2, 2), :, tx]
            return b["l2"].at[:, pl.ds(t * 4, 4), tx]

        for d in steps_4:
            for t in (core, other):
                tx = turned(x, d, 4)
                send(u, "lx", left_of(t, tx), b["dl"].at[:, xl, :, xh, core], device(tx, y, z, t))
        send(u, "lx", left_of(other, x), b["dl"].at[:, xl, :, xh, core], device(x, y, z, other))
        b["dl"][:, xl, :, xh, core] = left_of(core, x)[...]

        arrived(u, "rz")
        send(u, "swap", b["dr"], b["ds"], device(x, y, z, other))
        arrived(u, "lx")
        if u == 0:
            contract_outgoing(b, core, b["dr"])
            arrived(u, "swap")
            contract_outgoing(b, other, b["ds"])
        else:
            contract_incoming(b, core, b["dr"], False)
            arrived(u, "swap")
            contract_incoming(b, other, b["ds"], True)

        for d in steps_z:
            tz = turned(z, d, 8)
            send(u, "az", b["ta"].at[:, :, tz], b["a1"].at[z], device(x, y, tz, core))
        for d in (1, 3, 2, 0):
            for t in (core, other):
                tx = turned(x, d, 4)
                tl, th = lax.rem(tx, 2), lax.div(tx, 2)
                if d == 0 and t is core:
                    continue
                send(
                    u, "bx", b["tb"].at[:, tl, :, th, t],
                    b["b1"].at[pl.ds(core * 2, 2), x], device(tx, y, z, t),
                )
        b["a1"][z] = b["ta"][:, :, z]
        b["b1"][pl.ds(core * 2, 2), x] = b["tb"][:, xl, :, xh, core]

        arrived(u, "bx")
        for d in steps_4:
            ty = turned(y, d, 4)
            send(u, "by", b["b1"].at[ty], b["b2"].at[y], device(x, ty, z, core))
        b["b2"][y] = b["b1"][y]

        arrived(u, "az")
        for d in (1, 3, 2, 0):
            for t in (core, other):
                tx = turned(x, d, 4)
                tl, th = lax.rem(tx, 2), lax.div(tx, 2)
                if d == 0 and t is core:
                    continue
                send(
                    u, "ax", b["a1"].at[:, :, tl, th, t],
                    b["a2"].at[:, pl.ds(core * 2, 2), x], device(tx, y, z, t),
                )
        b["a2"][:, pl.ds(core * 2, 2), x] = b["a1"][:, :, xl, xh, core]

        arrived(u, "by")
        for d in steps_z:
            tz = turned(z, d, 8)
            send(u, "bz", b["b2"].at[:, :, tz], b["fb"].at[z], device(x, y, tz, core))
        b["fb"][z] = b["b2"][:, :, z]

        arrived(u, "ax")
        for d in steps_4:
            ty = turned(y, d, 4)
            send(u, "ay", b["a2"].at[:, ty], b["fa"].at[:, y], device(x, ty, z, core))
        b["fa"][:, y] = b["a2"][:, y]

        arrived(u, "ay")
        finish(u, b["fa"], 0, old, new)
        arrived(u, "bz")
        finish(u, b["fb"], 1, old, new)

    for u in range(2):
        for name in STAGES:
            descriptor(u, name).wait_send()


def local(pair_rep, proj_weight, gate_weight, out_weight, in_gain, out_gain):
    turned = jnp.transpose(pair_rep.reshape(128, 2, 16, 128), (3, 1, 2, 0)).reshape(128, 4096)
    vmem = pl.BlockSpec(memory_space=pltpu.VMEM)
    buffers = [
        pltpu.VMEM(shape, BF) for u in range(2) for shape in scratch_of(u).values()
    ]
    result = pl.pallas_call(
        kernel,
        out_shape=jax.ShapeDtypeStruct((128, 4096), BF),
        in_specs=[vmem] * 5 + [pl.BlockSpec(memory_space=pltpu.SMEM)],
        out_specs=vmem,
        scratch_shapes=buffers
        + [
            pltpu.VMEM((2, 6, 128, 128), BF),
            pltpu.VMEM((128, 4096), BF),
            pltpu.VMEM((128, 4096), F32),
            pltpu.VMEM((128, 4096), BF),
            pltpu.VMEM((128 * PITCH, 128), F32),
            pltpu.VMEM((512, 1024), BF),
            pltpu.VMEM((1024, 512), F32),
            pltpu.VMEM((128, 32, 128), BF),
            pltpu.SemaphoreType.DMA((2 * len(STAGES),)),
            pltpu.SemaphoreType.DMA((2 * len(STAGES),)),
        ],
        compiler_params=pltpu.CompilerParams(
            collective_id=0, has_side_effects=True, vmem_limit_bytes=60 * 1024 * 1024
        ),
    )(turned, proj_weight, gate_weight, out_weight, in_gain, out_gain)
    return jnp.transpose(result.reshape(128, 2, 16, 128), (3, 1, 2, 0)).reshape(128, 32, 128)


def solution(mesh):
    placed = (P("row", "col", None), P(), P(), P(), P(), P())
    return jax.shard_map(
        local, mesh=mesh, in_specs=placed, out_specs=P("row", "col", None), check_vma=False
    )
```

time: 536 us -> 201 us (0.38)
  waiting for transfers between devices: 367 us -> 0 us
  Pallas kernels: 0 us -> 192 us
  blocking collectives: 74.3 us -> 0 us
  starting transfers between devices: 32.5 us -> 0 us
  matrix products: 18.5 us -> 0 us
  local copies, waits for them, and re-layouts: 24.2 us -> 7.58 us
  between operations: 13.4 us -> 0.03 us
    pallas_call x0 -> x1, Pallas kernels: none -> 192 us  [local(): pl.pallas_call(kernel, out_shape=jax.ShapeDtypeStruct((128, 4096), BF), i...]
    all_gather x1 -> x0, waiting for transfers between devices: 143 us -> none  [local(): lax.all_gather(right_rows, ROW, axis=1, tiled=True)]
    all_to_all x4 -> x0, waiting for transfers between devices: 108 us -> none  [the longest x2 53.4 us: local(): lax.all_to_all(triangle.astype(jnp.bfloat16), 'col', split_axis=2, concat...]
    reduce_scatter x1 -> x0, waiting for transfers between devices: 80.3 us -> none  [sum_by_axis(): subtotal = lax.psum_scatter(subtotal, axis, scatter_dimension=0, tiled=True)]
    all_to_all x2 -> x0, blocking collectives: 74.3 us -> none  [the longest x1 40.6 us: local(): lax.all_to_all(right_hand, 'col', split_axis=0, concat_axis=2, tiled=True)]
    unnamed x4 -> x0, waiting for transfers between devices: 36.8 us -> none
    all_to_all x4 -> x0, starting transfers between devices: 32.4 us -> none  [the longest x2 20.5 us: local(): lax.all_to_all(triangle.astype(jnp.bfloat16), 'col', split_axis=2, concat...]
    dot_general x8 -> x0, matrix products: 18.5 us -> none  [the longest x1 5.71 us: local(): jnp.einsum('gik,gjk->igj', left_rows, lax.all_gather(right_rows, ROW, axi...]
  transfers between devices with their start and end apart: 7 -> 0, of which waited for: 7 -> 0; matrix products, arithmetic and copies ran while one was open for 1% -> 0% of each run, Pallas kernels for 0% -> 0%
where the time goes in v1:
time: 201 us; the launch traced here: 199 us
  Pallas kernels  192 us (96%)
  local copies, waits for them, and re-layouts  7.58 us (4%)
    pallas_call x1, Pallas kernels, local(): pl.pallas_call(kernel, out_shape=jax.ShapeDtypeStruct((128, 4096), BF), i...  192 us

profile of v1, /device:TPU:1, one launch (start us, length us, event | category | flops | bytes accessed | tf_op | source)
XLA Modules:
  0.0 199.1 jit_solution(13025690274864759132)
XLA Ops:
  0.0 2.5 %copy.7 = bf16[128,2,16,128]{0,2,1,3:T(8,128)(2,1)S(1)} copy(bf16[128,2,16,128]{3,2,1,0:T(8,128)(2,1)} %bitcast.17) | data formatting | bytes 2097152 | tf_op jit(solution)/shard_map/reshape | solution.py:363
  2.5 1.4 copy.12
  3.9 191.5 %shard_map.64 = bf16[128,4096]{1,0:T(8,128)(2,1)} custom-call(bf16[128,4096]{1,0:T(8,128)(2,1)} %bitcast.13, bf16[2,4,128,128]{3,2,1,0:T(8,128)(2,1)} %pw_ref.1, bf16[2,128,128]{2,1,0:T(8,128)(2,1)} %gw_ref.1, bf16[2,128,128]{2,1,0:T(8,128)(2,1)} %ow_ref.1, f32[2,128]{1,0:T(2,128)} %ig_ref.1, f32[2,128]{1,0:T(2,128)} %og_ref.1), custom_call_target="tpu_custom_call" | custom-call | tf_op jit(solution)/shard_map/pallas_call | solution.py:368
  195.4 1.4 copy.10
  196.9 2.3 %copy.8 = bf16[128,2,16,128]{3,2,1,0:T(8,128)(2,1)} copy(bf16[128,2,16,128]{0,2,1,3:T(8,128)(2,1)S(1)} %bitcast.15) | data formatting | bytes 2097152 | tf_op jit(solution)/shard_map/transpose | solution.py:390

commit v2 on v0

v2 whole, which is shorter than its diff:
```python
import jax
import jax.numpy as jnp
from jax import lax
from jax.experimental import pallas as pl
from jax.experimental.pallas import tpu as pltpu
from jax.sharding import PartitionSpec as P

EPS = 1e-05
MESH = pl.DeviceIdType.MESH
BF = jnp.bfloat16
F32 = jnp.float32
PITCH = 40
LANES = 512

FLOWS = ("first0", "first1", "swap", "last0", "last1", "tri0", "tri1")


def scratch_of(update):
    tile = (16, 128)
    return {
        "first": (128, 2) + tile,
        "last": (128, 2) + tile,
        "all_first": (8, 16, 2, 2) + tile,
        "all_last": ((4, 32, 2) if update == 0 else (8, 16, 2)) + tile,
        "tri": ((2, 4, 32) if update == 0 else (2, 8, 16)) + tile,
        "back": (2, 128) + tile,
    }


NAMES = tuple(scratch_of(0))


def kernel(x_ref, pw_ref, gw_ref, ow_ref, ig_ref, og_ref, out_ref, *scratch):
    count = len(NAMES)
    buffers = [dict(zip(NAMES, scratch[u * count : (u + 1) * count])) for u in range(2)]
    wt, norm, gate, state, stage, right_t, dummy, send_sem, recv_sem = scratch[2 * count :]

    row, col = lax.axis_index("row"), lax.axis_index("col")
    y, xl = lax.div(row, 2), lax.rem(row, 2)
    z, xh, core = lax.div(col, 4), lax.rem(lax.div(col, 2), 2), lax.rem(col, 2)
    x = xh * 2 + xl
    other = 1 - core
    channel = z * 16 + y * 4 + x
    chip_of_col = z * 2 + xh
    side = lax.div(y, 2)
    here_side = side == core

    def device(tx, ty, tz, tc):
        return (ty * 2 + lax.rem(tx, 2), tz * 4 + lax.div(tx, 2) * 2 + tc)

    barrier = pltpu.get_barrier_semaphore()

    @pl.loop(1, 256)
    def _(step):
        there = lax.rem(row * 32 + col + step, 256)
        pl.semaphore_signal(
            barrier, inc=1, device_id=(lax.div(there, 32), lax.rem(there, 32)), device_id_type=MESH
        )

    def copy(update, name, src, dst, target):
        index = update * len(FLOWS) + FLOWS.index(name)
        return pltpu.make_async_remote_copy(
            src_ref=src,
            dst_ref=dst,
            send_sem=send_sem.at[index],
            recv_sem=recv_sem.at[index],
            device_id=target,
            device_id_type=MESH,
        )

    def waits(update, name, kind):
        def wait(tiles):
            whole = dummy.at[pl.ds(0, tiles)]
            handle = copy(update, name, whole, whole, device(x, y, z, other))
            handle.wait_recv() if kind == "recv" else handle.wait_send()

        size = 2 if name.startswith("last") and update == 0 else 1
        if name == "swap":
            wait(256)
        elif update == 0 and not name.startswith("first"):

            @pl.when(here_side)
            def _():
                wait(127 * size)

            @pl.when(jnp.logical_not(here_side))
            def _():
                wait(128 * size)
        else:
            wait(127)

    def arrived(update, name):
        with jax.named_scope(f"wait_{name}_{update}"):
            waits(update, name, "recv")

    def far_first(step, size):
        if isinstance(step, int):
            return (size // 2 + ((step + 1) // 2 if step % 2 else -(step // 2))) % size
        half = lax.div(step + 1, 2)
        away = jnp.where(lax.rem(step, 2) == 1, half, -half)
        return lax.rem(size // 2 + away + size, size)

    def to_chips(one):
        @pl.loop(0, 16)
        def _(step):
            tx = lax.rem(x + far_first(lax.rem(step, 4), 4), 4)
            ty = lax.rem(y + far_first(lax.div(step, 4), 4), 4)
            for k in range(7):
                one(tx, ty, lax.rem(z + far_first(k, 8), 8))

        @pl.loop(0, 15)
        def _(step):
            tx = lax.rem(x + far_first(lax.rem(step, 4), 4), 4)
            ty = lax.rem(y + far_first(lax.div(step, 4), 4), 4)
            one(tx, ty, z)

    def send_same_core(update, name, which, half):
        b = buffers[update]
        landing = b["all_" + which]
        slot = landing.at[row, chip_of_col, core, half] if which == "first" else landing.at[row, chip_of_col, half]

        def one(tx, ty, tz):
            copy(
                update, name, b[which].at[tz * 16 + ty * 4 + tx, half], slot, device(tx, ty, tz, core)
            ).start()

        to_chips(one)
        slot[...] = b[which][channel, half]

    def send_left():
        b = buffers[0]
        slot = b["all_last"].at[lax.rem(row, 4), col]

        def one(tx, ty, tz):
            copy(
                0, "last0", b["last"].at[tz * 16 + ty * 4 + tx], slot, device(tx, ty, tz, side)
            ).start()

        to_chips(one)

        @pl.when(here_side)
        def _():
            slot[...] = b["last"][channel]

        @pl.when(jnp.logical_not(here_side))
        def _():
            one(x, y, z)

    def send_triangle(update, half):
        b = buffers[update]
        name = f"tri{half}"
        slot = b["back"].at[half, channel]
        if update == 1:

            def one(tx, ty, tz):
                src = b["tri"].at[half, ty * 2 + lax.rem(tx, 2), tz * 2 + lax.div(tx, 2)]
                copy(1, name, src, slot, device(tx, ty, tz, core)).start()

            to_chips(one)
            slot[...] = b["tri"][half, row, chip_of_col]
            return

        def one(tx, tq, tz, tc):
            src = b["tri"].at[half, tq * 2 + lax.rem(tx, 2), tz * 4 + lax.div(tx, 2) * 2 + tc]
            copy(0, name, src, slot, device(tx, core * 2 + tq, tz, tc)).start()

        def place(step):
            tx = lax.rem(x + far_first(lax.rem(lax.div(step, 2), 4), 4), 4)
            tq = lax.rem(y + 1 + lax.div(step, 8), 2)
            tc = lax.rem(core + 1 + lax.rem(step, 2), 2)
            return tx, tq, tc

        @pl.loop(0, 16)
        def _(step):
            tx, tq, tc = place(step)
            for k in range(7):
                one(tx, tq, lax.rem(z + far_first(k, 8), 8), tc)

        @pl.loop(0, 15)
        def _(step):
            tx, tq, tc = place(step)
            one(tx, tq, z, tc)

        @pl.when(here_side)
        def _():
            slot[...] = b["tri"][half, lax.rem(row, 4), col]

        @pl.when(jnp.logical_not(here_side))
        def _():
            one(x, lax.rem(y, 2), z, core)

    for u in range(2):
        for p in range(4):
            wt[u, p] = pw_ref[u, p].astype(F32).T.astype(BF)
        wt[u, 4] = gw_ref[u].astype(F32).T.astype(BF)
        wt[u, 5] = ow_ref[u].astype(F32).T.astype(BF)

    tiles = LANES // 128
    per_half = 2048 // LANES

    def lanes(step):
        return pl.ds(pl.multiple_of(step * LANES, LANES), LANES)

    def steps_of(half):
        return pl.loop(half * per_half, (half + 1) * per_half)

    def normalise(update, source, half):
        gain = jnp.broadcast_to(ig_ref[update : update + 1, :], (128, 128)).T
        gain = jnp.concatenate([gain] * tiles, axis=1)

        @steps_of(half)
        def _(step):
            wide = source[:, lanes(step)].astype(F32)
            center = wide - jnp.mean(wide, axis=0, keepdims=True)
            spread = jnp.mean(center * center, axis=0, keepdims=True)
            norm[:, lanes(step)] = (center * lax.rsqrt(spread + EPS) * gain).astype(BF)

    def project(update, hand, target, half):
        weight_gate, weight_value = wt[update, 2 * hand], wt[update, 2 * hand + 1]

        @steps_of(half)
        def _(step):
            normed = norm[:, lanes(step)]
            opening = jnp.dot(weight_gate, normed, preferred_element_type=F32)
            value = jnp.dot(weight_value, normed, preferred_element_type=F32)
            product = jax.nn.sigmoid(opening) * value
            for t in range(tiles):
                stage[pl.ds(step * tiles + t, 128, stride=PITCH), :] = product[:, t * 128 : (t + 1) * 128]

        @pl.loop(0, 8)
        def _(hz):
            for k in range(16):
                start = pl.multiple_of((hz * 16 + k) * PITCH + half * 16, 8)
                target[hz * 16 + k, half] = stage[pl.ds(start, 16), :].astype(BF)

    def gates(update, half):
        weight = wt[update, 4]

        @steps_of(half)
        def _(step):
            opening = jnp.dot(weight, norm[:, lanes(step)], preferred_element_type=F32)
            gate[:, lanes(step)] = jax.nn.sigmoid(opening)

    def turn_right():
        for jb in range(8):
            block = buffers[0]["all_first"][jb].reshape(1024, 128).T.reshape(4, 2, 16, 1024)
            for half in range(2):
                right_t[half, pl.ds(jb * 4, 4)] = block[:, half]

    def contract_outgoing(half):
        b = buffers[0]
        rows = right_t[half].reshape(512, 1024)
        for pair in range(2):
            operand = jnp.concatenate(
                [b["all_last"][pair * 2 + k].reshape(1024, 128) for k in range(2)], axis=1
            )
            product = jnp.dot(rows, operand, preferred_element_type=F32).astype(BF)
            for k in range(2):
                b["tri"][half, pair * 2 + k] = product[:, k * 128 : (k + 1) * 128].reshape(32, 16, 128)

    def contract_incoming(half):
        b = buffers[1]
        rows = jnp.concatenate([b["all_last"][k, :, half].reshape(256, 128) for k in range(8)], axis=1)
        for part in range(4):
            operand = jnp.concatenate(
                [b["all_first"][k, pl.ds(part * 4, 4)].reshape(256, 128) for k in range(8)], axis=1
            )
            product = lax.dot_general(
                rows, operand, (((1,), (1,)), ((), ())), preferred_element_type=F32
            ).astype(BF)
            for k in range(2):
                b["tri"][half, part * 2 + k] = product[:, k * 128 : (k + 1) * 128].reshape(16, 16, 128)

    def finish(update, half, old, new):
        source = buffers[update]["back"]

        def total(read):
            def add(hz, running):
                for k in range(16):
                    running = running + read(hz * 16 + k)
                return running

            return lax.fori_loop(0, 8, add, jnp.zeros((16, 128), F32))

        mean = total(lambda h: source[half, h].astype(F32)) * (1.0 / 128)

        def square(h):
            center = source[half, h].astype(F32) - mean
            return center * center

        inverse = lax.rsqrt(total(square) * (1.0 / 128) + EPS)

        @pl.loop(0, 8)
        def _(hz):
            for k in range(16):
                h = hz * 16 + k
                mixed = (source[half, h].astype(F32) - mean) * inverse * og_ref[update, h]
                stage[pl.ds(pl.multiple_of(h * PITCH, 8), 16), :] = mixed

        weight = wt[update, 5]

        for step in range(per_half):
            mixed = jnp.concatenate(
                [stage[pl.ds(step * tiles + t, 128, stride=PITCH), :] for t in range(tiles)], axis=1
            ).astype(BF)
            change = jnp.dot(weight, mixed, preferred_element_type=F32)
            here = pl.ds(half * 2048 + step * LANES, LANES)
            new[:, here] = (old[:, here].astype(F32) + gate[:, here] * change).astype(BF)

    b = buffers[0]
    for half in range(2):
        normalise(0, x_ref, half)
        project(0, 1, b["first"], half)
        if half == 0:
            with jax.named_scope("barrier"):
                pl.semaphore_wait(barrier, 255)
        with jax.named_scope("send_first"):
            send_same_core(0, f"first{half}", "first", half)
    for half in range(2):
        project(0, 0, b["last"], half)
    with jax.named_scope("send_last"):
        send_left()
    for half in range(2):
        gates(0, half)

    def exchange(update):
        landing = buffers[update]["all_first"]
        for half in range(2):
            arrived(update, f"first{half}")
        own = landing.at[:, :, core]
        copy(update, "swap", own, own, device(x, y, z, other)).start()
        arrived(update, "swap")

    exchange(0)
    with jax.named_scope("turn_right"):
        turn_right()
    arrived(0, "last0")
    for half in range(2):
        with jax.named_scope("contract"):
            contract_outgoing(half)
        with jax.named_scope("send_tri"):
            send_triangle(0, half)

    b = buffers[1]
    for half in range(2):
        arrived(0, f"tri{half}")
        with jax.named_scope("finish"):
            finish(0, half, x_ref, state)
        with jax.named_scope("project"):
            normalise(1, state, half)
            project(1, 0, b["first"], half)
        with jax.named_scope("send_first"):
            send_same_core(1, f"first{half}", "first", half)
    for half in range(2):
        with jax.named_scope("project"):
            project(1, 1, b["last"], half)
        with jax.named_scope("send_last"):
            send_same_core(1, f"last{half}", "last", half)
    for half in range(2):
        gates(1, half)
    exchange(1)
    for half in range(2):
        arrived(1, f"last{half}")
        with jax.named_scope("contract"):
            contract_incoming(half)
        with jax.named_scope("send_tri"):
            send_triangle(1, half)
    for half in range(2):
        arrived(1, f"tri{half}")
        with jax.named_scope("finish"):
            finish(1, half, state, out_ref)

    for u in range(2):
        for name in FLOWS:
            if (u, name) != (0, "last1"):
                waits(u, name, "send")


def local(pair_rep, proj_weight, gate_weight, out_weight, in_gain, out_gain):
    turned = jnp.transpose(pair_rep, (2, 1, 0)).reshape(128, 4096)
    vmem = pl.BlockSpec(memory_space=pltpu.VMEM)
    buffers = [pltpu.VMEM(shape, BF) for u in range(2) for shape in scratch_of(u).values()]
    result = pl.pallas_call(
        kernel,
        out_shape=jax.ShapeDtypeStruct((128, 4096), BF),
        in_specs=[vmem] * 5 + [pl.BlockSpec(memory_space=pltpu.SMEM)],
        out_specs=vmem,
        scratch_shapes=buffers
        + [
            pltpu.VMEM((2, 6, 128, 128), BF),
            pltpu.VMEM((128, 4096), BF),
            pltpu.VMEM((128, 4096), F32),
            pltpu.VMEM((128, 4096), BF),
            pltpu.VMEM((128 * PITCH, 128), F32),
            pltpu.VMEM((2, 32, 16, 1024), BF),
            pltpu.VMEM((256, 16, 128), BF),
            pltpu.SemaphoreType.DMA((2 * len(FLOWS),)),
            pltpu.SemaphoreType.DMA((2 * len(FLOWS),)),
        ],
        compiler_params=pltpu.CompilerParams(
            collective_id=0, has_side_effects=True, vmem_limit_bytes=56 * 1024 * 1024
        ),
    )(turned, proj_weight, gate_weight, out_weight, in_gain, out_gain)
    return jnp.transpose(result.reshape(128, 32, 128), (2, 1, 0))


def solution(mesh):
    placed = (P("row", "col", None), P(), P(), P(), P(), P())
    return jax.shard_map(
        local, mesh=mesh, in_specs=placed, out_specs=P("row", "col", None), check_vma=False
    )
```

time: 536 us -> 164 us (0.31)
  waiting for transfers between devices: 367 us -> 0 us
  Pallas kernels: 0 us -> 157 us
  blocking collectives: 74.3 us -> 0 us
  starting transfers between devices: 32.5 us -> 0 us
  matrix products: 18.5 us -> 0 us
  local copies, waits for them, and re-layouts: 24.2 us -> 7.58 us
  between operations: 13.4 us -> 0.03 us
    pallas_call x0 -> x1, Pallas kernels: none -> 157 us  [local(): pl.pallas_call(kernel, out_shape=jax.ShapeDtypeStruct((128, 4096), BF), i...]
    all_gather x1 -> x0, waiting for transfers between devices: 143 us -> none  [local(): lax.all_gather(right_rows, ROW, axis=1, tiled=True)]
    all_to_all x4 -> x0, waiting for transfers between devices: 108 us -> none  [the longest x2 53.4 us: local(): lax.all_to_all(triangle.astype(jnp.bfloat16), 'col', split_axis=2, concat...]
    reduce_scatter x1 -> x0, waiting for transfers between devices: 80.3 us -> none  [sum_by_axis(): subtotal = lax.psum_scatter(subtotal, axis, scatter_dimension=0, tiled=True)]
    all_to_all x2 -> x0, blocking collectives: 74.3 us -> none  [the longest x1 40.6 us: local(): lax.all_to_all(right_hand, 'col', split_axis=0, concat_axis=2, tiled=True)]
    unnamed x4 -> x0, waiting for transfers between devices: 36.8 us -> none
    all_to_all x4 -> x0, starting transfers between devices: 32.4 us -> none  [the longest x2 20.5 us: local(): lax.all_to_all(triangle.astype(jnp.bfloat16), 'col', split_axis=2, concat...]
    dot_general x8 -> x0, matrix products: 18.5 us -> none  [the longest x1 5.71 us: local(): jnp.einsum('gik,gjk->igj', left_rows, lax.all_gather(right_rows, ROW, axi...]
  transfers between devices with their start and end apart: 7 -> 0, of which waited for: 7 -> 0; matrix products, arithmetic and copies ran while one was open for 1% -> 0% of each run, Pallas kernels for 0% -> 0%
where the time goes in v2:
time: 164 us
  Pallas kernels  157 us (96%)
  local copies, waits for them, and re-layouts  7.58 us (5%)
    pallas_call x1, Pallas kernels, local(): pl.pallas_call(kernel, out_shape=jax.ShapeDtypeStruct((128, 4096), BF), i...  157 us

profile of v2, /device:TPU:1, one launch (start us, length us, event | category | flops | bytes accessed | tf_op | source)
XLA Modules:
  0.0 164.3 jit_solution(3515933181275623711)
XLA Ops:
  0.0 2.5 %copy.7 = bf16[128,32,128]{2,1,0:T(8,128)(2,1)S(1)} copy(bf16[128,32,128]{0,1,2:T(8,128)(2,1)} %bitcast.12) | data formatting | bytes 2097152 | tf_op jit(solution)/shard_map/transpose | solution.py:380
  2.5 1.4 copy.12
  3.9 156.6 %shard_map.64 = bf16[128,4096]{1,0:T(8,128)(2,1)} custom-call(bf16[128,4096]{1,0:T(8,128)(2,1)} %bitcast.8, bf16[2,4,128,128]{3,2,1,0:T(8,128)(2,1)} %pw_ref.1, bf16[2,128,128]{2,1,0:T(8,128)(2,1)} %gw_ref.1, bf16[2,128,128]{2,1,0:T(8,128)(2,1)} %ow_ref.1, f32[2,128]{1,0:T(2,128)} %ig_ref.1, f32[2,128]{1,0:T(2,128)} %og_ref.1), custom_call_target="tpu_custom_call" | custom-call | tf_op jit(solution)/shard_map/pallas_call | solution.py:383
  160.5 1.4 copy.10
  162.0 2.3 %copy.8 = bf16[128,32,128]{0,1,2:T(8,128)(2,1)} copy(bf16[128,32,128]{2,1,0:T(8,128)(2,1)S(1)} %bitcast.10) | data formatting | bytes 2097152 | tf_op jit(solution)/shard_map/reshape | solution.py:404

commit v3 on v2

v3 whole, which is shorter than its diff:
```python
import jax
import jax.numpy as jnp
from jax import lax
from jax.experimental import pallas as pl
from jax.experimental.pallas import tpu as pltpu
from jax.sharding import PartitionSpec as P

EPS = 1e-05
MESH = pl.DeviceIdType.MESH
BF = jnp.bfloat16
F32 = jnp.float32
PITCH = 40
LANES = 512

FLOWS = ("first0", "first1", "swap", "last0", "last1", "tri0", "tri1")
FAR_COLS = sorted(range(32), key=lambda c: -min(c, 32 - c))


def scratch_of(update):
    tile = (16, 128)
    return {
        "first": (128, 2) + tile,
        "last": (128, 2) + tile,
        "all_first": (4, 2, 16, 2, 2) + tile,
        "all_last": ((2, 2, 32, 2) if update == 0 else (8, 16, 2)) + tile,
        "tri": ((2, 2, 2, 32) if update == 0 else (2, 8, 16)) + tile,
        "back": (2, 128) + tile,
    }


NAMES = tuple(scratch_of(0))


def kernel(x_in, pw_in, gw_in, ow_in, ig_in, og_in, out_ref, *scratch):
    count = len(NAMES)
    buffers = [dict(zip(NAMES, scratch[u * count : (u + 1) * count])) for u in range(2)]
    (wt, norm, gate, start, state, stage, right_t, dummy, send_sem, recv_sem) = scratch[2 * count : -7]
    x_ref, pw_ref, gw_ref, ow_ref, ig_ref, og_ref, local_sem = scratch[-7:]
    loads = [
        pltpu.make_async_copy(src, dst, local_sem.at[k])
        for k, (src, dst) in enumerate(
            ((x_in, x_ref), (pw_in, pw_ref), (ig_in, ig_ref), (gw_in, gw_ref), (ow_in, ow_ref), (og_in, og_ref))
        )
    ]
    for load in loads:
        load.start()

    row, col = lax.axis_index("row"), lax.axis_index("col")
    y, xl = lax.div(row, 2), lax.rem(row, 2)
    z, xh, core = lax.div(col, 4), lax.rem(lax.div(col, 2), 2), lax.rem(col, 2)
    x = xh * 2 + xl
    other = 1 - core
    channel = z * 16 + y * 4 + x
    chip_of_col = z * 2 + xh
    side = lax.div(y, 2)
    here_side = side == core

    def device(tx, ty, tz, tc):
        return (ty * 2 + lax.rem(tx, 2), tz * 4 + lax.div(tx, 2) * 2 + tc)

    barrier = pltpu.get_barrier_semaphore()

    def greet(to_row, to_col):
        pl.semaphore_signal(barrier, inc=1, device_id=(to_row, to_col), device_id_type=MESH)

    @pl.loop(0, 7)
    def _(step):
        half = lax.div(step + 1, 2)
        to_row = lax.rem(row + 12 + jnp.where(lax.rem(step, 2) == 1, half, -half), 8)
        for away in FAR_COLS:
            greet(to_row, lax.rem(col + away, 32))

    for away in FAR_COLS[:-1]:
        greet(row, lax.rem(col + away, 32))

    def copy(update, name, src, dst, target):
        index = update * len(FLOWS) + FLOWS.index(name)
        return pltpu.make_async_remote_copy(
            src_ref=src,
            dst_ref=dst,
            send_sem=send_sem.at[index],
            recv_sem=recv_sem.at[index],
            device_id=target,
            device_id_type=MESH,
        )

    def waits(update, name, kind):
        def wait(tiles):
            whole = dummy.at[pl.ds(0, tiles)]
            handle = copy(update, name, whole, whole, device(x, y, z, other))
            handle.wait_recv() if kind == "recv" else handle.wait_send()

        def wait_less(tiles, own, less):
            @pl.when(own)
            def _():
                wait(tiles - less)

            @pl.when(jnp.logical_not(own))
            def _():
                wait(tiles)

        if name == "swap":
            wait(256)
        elif update == 0 and not name.startswith("first"):
            wait_less(128, here_side, 1)
        else:
            wait(127)

    def arrived(update, name):
        with jax.named_scope(f"wait_{name}_{update}"):
            waits(update, name, "recv")

    def far_first(step, size):
        if isinstance(step, int):
            return (size // 2 + ((step + 1) // 2 if step % 2 else -(step // 2))) % size
        half = lax.div(step + 1, 2)
        away = jnp.where(lax.rem(step, 2) == 1, half, -half)
        return lax.rem(size // 2 + away + size, size)

    def to_chips(one):
        @pl.loop(0, 16)
        def _(step):
            tx = lax.rem(x + far_first(lax.rem(step, 4), 4), 4)
            ty = lax.rem(y + far_first(lax.div(step, 4), 4), 4)
            for k in range(7):
                one(tx, ty, lax.rem(z + far_first(k, 8), 8))

        @pl.loop(0, 15)
        def _(step):
            tx = lax.rem(x + far_first(lax.rem(step, 4), 4), 4)
            ty = lax.rem(y + far_first(lax.div(step, 4), 4), 4)
            one(tx, ty, z)

    def send_same_core(update, name, which, source, half):
        landing = buffers[update]["all_" + which]
        if which == "first":
            slot = landing.at[y, xl, chip_of_col, core, half]
        else:
            slot = landing.at[row, chip_of_col, half]

        def one(tx, ty, tz):
            copy(
                update, name, source.at[tz * 16 + ty * 4 + tx, half], slot, device(tx, ty, tz, core)
            ).start()

        to_chips(one)
        slot[...] = source[channel, half]

    def send_left(name, source, half):
        slot = buffers[0]["all_last"].at[lax.rem(y, 2), xl, col, half]

        def one(tx, ty, tz):
            copy(
                0, name, source.at[tz * 16 + ty * 4 + tx, half], slot, device(tx, ty, tz, side)
            ).start()

        to_chips(one)

        @pl.when(here_side)
        def _():
            slot[...] = source[channel, half]

        @pl.when(jnp.logical_not(here_side))
        def _():
            one(x, y, z)

    def send_rows(half, yq):
        b = buffers[0]
        slot = b["back"].at[half, channel]

        def one(tx, tz, tc):
            src = b["tri"].at[half, yq, lax.rem(tx, 2), tz * 4 + lax.div(tx, 2) * 2 + tc]
            copy(0, f"tri{half}", src, slot, device(tx, core * 2 + yq, tz, tc)).start()

        def place(step):
            tx = lax.rem(x + far_first(lax.div(step, 2), 4), 4)
            return tx, lax.rem(core + 1 + lax.rem(step, 2), 2)

        @pl.loop(0, 8)
        def _(step):
            tx, tc = place(step)
            for k in range(7):
                one(tx, lax.rem(z + far_first(k, 8), 8), tc)

        for step in range(7):
            tx, tc = place(step)
            one(tx, z, tc)
        own = jnp.logical_and(here_side, lax.rem(y, 2) == yq)

        @pl.when(own)
        def _():
            slot[...] = b["tri"][half, yq, xl, col]

        @pl.when(jnp.logical_not(own))
        def _():
            one(x, z, core)

    def send_triangle(half):
        b = buffers[1]
        slot = b["back"].at[half, channel]

        def one(tx, ty, tz):
            src = b["tri"].at[half, ty * 2 + lax.rem(tx, 2), tz * 2 + lax.div(tx, 2)]
            copy(1, f"tri{half}", src, slot, device(tx, ty, tz, core)).start()

        to_chips(one)
        slot[...] = b["tri"][half, row, chip_of_col]

    def turn_weight(update, index, weight):
        wt[update, index] = weight.astype(F32).T.astype(BF)

    tiles = LANES // 128
    per_half = 2048 // LANES

    def lanes(step):
        return pl.ds(pl.multiple_of(step * LANES, LANES), LANES)

    def steps_of(half):
        return pl.loop(half * per_half, (half + 1) * per_half)

    def load(half):
        rows = pl.ds(half * 16, 16)

        @pl.loop(0, 16)
        def _(step):
            for k in range(8):
                i = step * 8 + k
                stage[pl.ds(pl.multiple_of(i * PITCH + half * 16, 8), 16), :] = x_ref[i, rows, :].astype(F32)

        @steps_of(half)
        def _(step):
            for t in range(tiles):
                block = stage[pl.ds(step * tiles + t, 128, stride=PITCH), :]
                lane = pl.multiple_of(step * LANES + t * 128, 128)
                start[:, pl.ds(lane, 128)] = block.T.astype(BF)

    def normalise(update, source, half):
        gain = jnp.broadcast_to(ig_ref[update : update + 1, :], (128, 128)).T
        gain = jnp.concatenate([gain] * tiles, axis=1)

        @steps_of(half)
        def _(step):
            wide = source[:, lanes(step)].astype(F32)
            center = wide - jnp.mean(wide, axis=0, keepdims=True)
            spread = jnp.mean(center * center, axis=0, keepdims=True)
            norm[:, lanes(step)] = (center * lax.rsqrt(spread + EPS) * gain).astype(BF)

    def project(update, hand, target, half):
        weight_gate, weight_value = wt[update, 2 * hand], wt[update, 2 * hand + 1]

        @steps_of(half)
        def _(step):
            normed = norm[:, lanes(step)]
            opening = jnp.dot(weight_gate, normed, preferred_element_type=F32)
            value = jnp.dot(weight_value, normed, preferred_element_type=F32)
            product = jax.nn.sigmoid(opening) * value
            for t in range(tiles):
                stage[pl.ds(step * tiles + t, 128, stride=PITCH), :] = product[:, t * 128 : (t + 1) * 128]

        @pl.loop(0, 8)
        def _(hz):
            for k in range(16):
                start = pl.multiple_of((hz * 16 + k) * PITCH + half * 16, 8)
                target[hz * 16 + k, half] = stage[pl.ds(start, 16), :].astype(BF)

    def gates(update, half):
        weight = wt[update, 4]

        @steps_of(half)
        def _(step):
            opening = jnp.dot(weight, norm[:, lanes(step)], preferred_element_type=F32)
            gate[:, lanes(step)] = jax.nn.sigmoid(opening)

    def turn_right():
        for jb in range(8):
            block = buffers[0]["all_first"][jb // 2, jb % 2].reshape(1024, 128).T.reshape(4, 2, 16, 1024)
            for half in range(2):
                right_t[half, pl.ds(jb * 4, 4)] = block[:, half]

    def contract_outgoing(half, yq):
        b = buffers[0]
        rows = right_t[half].reshape(512, 1024)
        operand = jnp.concatenate([b["all_last"][yq, k].reshape(1024, 128) for k in range(2)], axis=1)
        product = jnp.dot(rows, operand, preferred_element_type=F32).astype(BF)
        for k in range(2):
            b["tri"][half, yq, k] = product[:, k * 128 : (k + 1) * 128].reshape(32, 16, 128)

    def contract_incoming(half):
        b = buffers[1]
        rows = jnp.concatenate([b["all_last"][k, :, half].reshape(256, 128) for k in range(8)], axis=1)
        for part in range(4):
            operand = jnp.concatenate(
                [
                    b["all_first"][k // 2, k % 2, pl.ds(part * 4, 4)].reshape(256, 128)
                    for k in range(8)
                ],
                axis=1,
            )
            product = lax.dot_general(
                rows, operand, (((1,), (1,)), ((), ())), preferred_element_type=F32
            ).astype(BF)
            for k in range(2):
                b["tri"][half, part * 2 + k] = product[:, k * 128 : (k + 1) * 128].reshape(16, 16, 128)

    def finish(update, half, old):
        source = buffers[update]["back"]

        def total(read):
            def add(hz, running):
                for k in range(16):
                    running = running + read(hz * 16 + k)
                return running

            return lax.fori_loop(0, 8, add, jnp.zeros((16, 128), F32))

        mean = total(lambda h: source[half, h].astype(F32)) * (1.0 / 128)

        def square(h):
            center = source[half, h].astype(F32) - mean
            return center * center

        inverse = lax.rsqrt(total(square) * (1.0 / 128) + EPS)

        @pl.loop(0, 8)
        def _(hz):
            for k in range(16):
                h = hz * 16 + k
                mixed = (source[half, h].astype(F32) - mean) * inverse * og_ref[update, h]
                stage[pl.ds(pl.multiple_of(h * PITCH + half * 16, 8), 16), :] = mixed

        weight = wt[update, 5]

        for step in range(per_half):
            mixed = jnp.concatenate(
                [
                    stage[pl.ds(half * 16 + step * tiles + t, 128, stride=PITCH), :]
                    for t in range(tiles)
                ],
                axis=1,
            ).astype(BF)
            change = jnp.dot(weight, mixed, preferred_element_type=F32)
            here = pl.ds(half * 2048 + step * LANES, LANES)
            total_here = old[:, here].astype(F32) + gate[:, here] * change
            if update == 0:
                state[:, here] = total_here.astype(BF)
                continue
            for t in range(tiles):
                row_of_j = half * 16 + step * tiles + t
                stage[pl.ds(row_of_j, 128, stride=PITCH), :] = total_here[:, t * 128 : (t + 1) * 128].T
        if update == 1:
            rows = pl.ds(half * 16, 16)

            @pl.loop(0, 16)
            def _(step):
                for k in range(8):
                    i = step * 8 + k
                    begin = pl.multiple_of(i * PITCH + half * 16, 8)
                    out_ref[i, rows, :] = stage[pl.ds(begin, 16), :].astype(BF)

    def scope(name, run, *args):
        with jax.named_scope(name):
            run(*args)

    b = buffers[0]
    for k in range(3):
        loads[k].wait()
    for p in range(4):
        turn_weight(0, p, pw_ref[0, p])
    for half in range(2):
        scope("load", load, half)
        scope("normalise", normalise, 0, start, half)
        scope("project", project, 0, 1, b["first"], half)
        if half == 0:
            with jax.named_scope("barrier"):
                pl.semaphore_wait(barrier, 255)
        scope("send_first", send_same_core, 0, f"first{half}", "first", b["first"], half)
    for half in range(2):
        scope("project", project, 0, 0, b["last"], half)
        scope("send_last", send_left, f"last{half}", b["last"], half)
    for k in range(3, 6):
        loads[k].wait()
    for u in range(2):
        if u == 1:
            for p in range(4):
                turn_weight(1, p, pw_ref[1, p])
        turn_weight(u, 4, gw_ref[u])
        turn_weight(u, 5, ow_ref[u])
    for half in range(2):
        scope("gates", gates, 0, half)

    def exchange(update):
        for half in range(2):
            arrived(update, f"first{half}")
        own = buffers[update]["all_first"].at[:, :, :, core]
        copy(update, "swap", own, own, device(x, y, z, other)).start()
        arrived(update, "swap")

    exchange(0)
    scope("turn_right", turn_right)
    for half in range(2):
        arrived(0, f"last{half}")
    for half in range(2):
        for yq in range(2):
            scope("contract", contract_outgoing, half, yq)
            scope("send_tri", send_rows, half, yq)

    b = buffers[1]
    for half in range(2):
        arrived(0, f"tri{half}")
        scope("finish", finish, 0, half, start)
        scope("normalise", normalise, 1, state, half)
        scope("project", project, 1, 0, b["first"], half)
        scope("send_first", send_same_core, 1, f"first{half}", "first", b["first"], half)
    for half in range(2):
        scope("project", project, 1, 1, b["last"], half)
        scope("send_last", send_same_core, 1, f"last{half}", "last", b["last"], half)
    for half in range(2):
        scope("gates", gates, 1, half)
    exchange(1)
    for half in range(2):
        arrived(1, f"last{half}")
        scope("contract", contract_incoming, half)
        scope("send_tri", send_triangle, half)
    for half in range(2):
        arrived(1, f"tri{half}")
        scope("finish", finish, 1, half, state)

    for u in range(2):
        for name in FLOWS:
            waits(u, name, "send")


def local(pair_rep, proj_weight, gate_weight, out_weight, in_gain, out_gain):
    inputs = [
        pltpu.with_memory_space_constraint(array, pltpu.HBM)
        for array in (pair_rep, proj_weight, gate_weight, out_weight, in_gain, out_gain)
    ]
    buffers = [pltpu.VMEM(shape, BF) for u in range(2) for shape in scratch_of(u).values()]
    return pl.pallas_call(
        kernel,
        out_shape=jax.ShapeDtypeStruct((128, 32, 128), BF),
        in_specs=[pl.BlockSpec(memory_space=pltpu.HBM)] * 6,
        out_specs=pl.BlockSpec(memory_space=pltpu.VMEM),
        scratch_shapes=buffers
        + [
            pltpu.VMEM((2, 6, 128, 128), BF),
            pltpu.VMEM((128, 4096), BF),
            pltpu.VMEM((128, 4096), F32),
            pltpu.VMEM((128, 4096), BF),
            pltpu.VMEM((128, 4096), BF),
            pltpu.VMEM((128 * PITCH, 128), F32),
            pltpu.VMEM((2, 32, 16, 1024), BF),
            pltpu.VMEM((256, 16, 128), BF),
            pltpu.SemaphoreType.DMA((2 * len(FLOWS),)),
            pltpu.SemaphoreType.DMA((2 * len(FLOWS),)),
            pltpu.VMEM((128, 32, 128), BF),
            pltpu.VMEM((2, 4, 128, 128), BF),
            pltpu.VMEM((2, 128, 128), BF),
            pltpu.VMEM((2, 128, 128), BF),
            pltpu.VMEM((2, 128), F32),
            pltpu.SMEM((2, 128), F32),
            pltpu.SemaphoreType.DMA((6,)),
        ],
        compiler_params=pltpu.CompilerParams(
            collective_id=0, has_side_effects=True, vmem_limit_bytes=36 * 1024 * 1024
        ),
    )(*inputs)


def solution(mesh):
    placed = (P("row", "col", None), P(), P(), P(), P(), P())
    return jax.shard_map(
        local, mesh=mesh, in_specs=placed, out_specs=P("row", "col", None), check_vma=False
    )
```

time: 164 us -> 157 us (0.957)
  local copies, waits for them, and re-layouts: 7.58 us -> 0.97 us
  Pallas kernels: 157 us -> 155 us
    transpose x1 -> x0, local copies, waits for them, and re-layouts: 2.47 us -> none  [local(): turned = jnp.transpose(pair_rep, (2, 1, 0)).reshape(128, 4096)]
    reshape x1 -> x0, local copies, waits for them, and re-layouts: 2.26 us -> none  [local(): return jnp.transpose(result.reshape(128, 32, 128), (2, 1, 0))]
    unnamed x2 -> x1, local copies, waits for them, and re-layouts: 2.86 us -> 0.97 us
where the time goes in v3:
time: 157 us; the launch traced here: 156 us
  Pallas kernels  155 us (99%)
    pallas_call x1, Pallas kernels, local(): pl.pallas_call(kernel, out_shape=jax.ShapeDtypeStruct((128, 32, 128), BF)...  155 us

profile of v3, /device:TPU:1, one launch (start us, length us, event | category | flops | bytes accessed | tf_op | source)
XLA Modules:
  0.0 156.4 jit_solution(15892326813983079195)
XLA Ops:
  0.0 155.4 %shard_map.64 = bf16[128,32,128]{2,1,0:T(8,128)(2,1)S(1)} custom-call(bf16[128,32,128]{2,1,0:T(8,128)(2,1)} %x_in.1, bf16[2,4,128,128]{3,2,1,0:T(8,128)(2,1)} %pw_in.1, bf16[2,128,128]{2,1,0:T(8,128)(2,1)} %gw_in.1, bf16[2,128,128]{2,1,0:T(8,128)(2,1)} %ow_in.1, f32[2,128]{1,0:T(2,128)} %ig_in.1, f32[2,128]{1,0:T(2,128)} %og_in.1), custom_call_target="tpu_custom_call" | custom-call | tf_op jit(solution)/shard_map/pallas_call | solution.py:439
  155.4 1.0 copy.8

commit v4 on v3

--- a/solution.py
+++ b/solution.py
@@ -13,7 +13,6 @@
 LANES = 512
 
 FLOWS = ("first0", "first1", "swap", "last0", "last1", "tri0", "tri1")
-FAR_COLS = sorted(range(32), key=lambda c: -min(c, 32 - c))
 
 
 def scratch_of(update):
@@ -34,7 +33,7 @@
 def kernel(x_in, pw_in, gw_in, ow_in, ig_in, og_in, out_ref, *scratch):
     count = len(NAMES)
     buffers = [dict(zip(NAMES, scratch[u * count : (u + 1) * count])) for u in range(2)]
-    (wt, norm, gate, start, state, stage, right_t, dummy, send_sem, recv_sem) = scratch[2 * count : -7]
+    (wt, norm, gate, start, state, stage, right_t, left_n, dummy, send_sem, recv_sem) = scratch[2 * count : -7]
     x_ref, pw_ref, gw_ref, ow_ref, ig_ref, og_ref, local_sem = scratch[-7:]
     loads = [
         pltpu.make_async_copy(src, dst, local_sem.at[k])
@@ -42,8 +41,8 @@
             ((x_in, x_ref), (pw_in, pw_ref), (ig_in, ig_ref), (gw_in, gw_ref), (ow_in, ow_ref), (og_in, og_ref))
         )
     ]
-    for load in loads:
-        load.start()
+    for k in range(3):
+        loads[k].start()
 
     row, col = lax.axis_index("row"), lax.axis_index("col")
     y, xl = lax.div(row, 2), lax.rem(row, 2)
@@ -58,20 +57,31 @@
     def device(tx, ty, tz, tc):
         return (ty * 2 + lax.rem(tx, 2), tz * 4 + lax.div(tx, 2) * 2 + tc)
 
+    def far_first(step, size):
+        if isinstance(step, int):
+            return (size // 2 + ((step + 1) // 2 if step % 2 else -(step // 2))) % size
+        half = lax.div(step + 1, 2)
+        away = jnp.where(lax.rem(step, 2) == 1, half, -half)
+        return lax.rem(size // 2 + away + size, size)
+
     barrier = pltpu.get_barrier_semaphore()
 
     def greet(to_row, to_col):
         pl.semaphore_signal(barrier, inc=1, device_id=(to_row, to_col), device_id_type=MESH)
 
-    @pl.loop(0, 7)
+    far_rows = [lax.rem(row + away, 8) for away in (4, 3, 5, 2, 6, 1, 7, 0)]
+
+    @pl.loop(0, 31)
     def _(step):
-        half = lax.div(step + 1, 2)
-        to_row = lax.rem(row + 12 + jnp.where(lax.rem(step, 2) == 1, half, -half), 8)
-        for away in FAR_COLS:
-            greet(to_row, lax.rem(col + away, 32))
-
-    for away in FAR_COLS[:-1]:
-        greet(row, lax.rem(col + away, 32))
+        to_col = lax.rem(col + far_first(step, 32), 32)
+        for to_row in far_rows:
+            greet(to_row, to_col)
+
+    for to_row in far_rows[:-1]:
+        greet(to_row, col)
+
+    for k in range(3, 6):
+        loads[k].start()
 
     def copy(update, name, src, dst, target):
         index = update * len(FLOWS) + FLOWS.index(name)
@@ -110,13 +120,6 @@
         with jax.named_scope(f"wait_{name}_{update}"):
             waits(update, name, "recv")
 
-    def far_first(step, size):
-        if isinstance(step, int):
-            return (size // 2 + ((step + 1) // 2 if step % 2 else -(step // 2))) % size
-        half = lax.div(step + 1, 2)
-        away = jnp.where(lax.rem(step, 2) == 1, half, -half)
-        return lax.rem(size // 2 + away + size, size)
-
     def to_chips(one):
         @pl.loop(0, 16)
         def _(step):
@@ -218,21 +221,37 @@
     def steps_of(half):
         return pl.loop(half * per_half, (half + 1) * per_half)
 
+    def halves_of_lanes(first, second):
+        return [
+            jnp.concatenate([first[..., k : k + 64], second[..., k : k + 64]], axis=-1) for k in (0, 64)
+        ]
+
     def load(half):
-        rows = pl.ds(half * 16, 16)
-
-        @pl.loop(0, 16)
+        @pl.loop(0, 8)
         def _(step):
             for k in range(8):
-                i = step * 8 + k
-                stage[pl.ds(pl.multiple_of(i * PITCH + half * 16, 8), 16), :] = x_ref[i, rows, :].astype(F32)
-
-        @steps_of(half)
-        def _(step):
-            for t in range(tiles):
-                block = stage[pl.ds(step * tiles + t, 128, stride=PITCH), :]
-                lane = pl.multiple_of(step * LANES + t * 128, 128)
+                i = half * 64 + step * 8 + k
+                stage[pl.ds(pl.multiple_of(i * PITCH, 8), 32), :] = x_ref[i].astype(F32)
+
+        @pl.loop(0, 4)
+        def _(step):
+            for t in range(4):
+                j = step * 4 + t
+                block = jnp.concatenate(
+                    [
+                        stage[pl.ds(half * 64 * PITCH + k * 16 + j, 64, stride=PITCH), :]
+                        for k in range(2)
+                    ],
+                    axis=0,
+                )
+                lane = pl.multiple_of(half * 2048 + j * 128, 128)
                 start[:, pl.ds(lane, 128)] = block.T.astype(BF)
+
+    def unfold():
+        for j in range(16):
+            tiles_of_j = [state[:, pl.ds((half * 16 + j) * 128, 128)] for half in range(2)]
+            for k, tile in enumerate(halves_of_lanes(*tiles_of_j)):
+                start[:, pl.ds((k * 16 + j) * 128, 128)] = tile
 
     def normalise(update, source, half):
         gain = jnp.broadcast_to(ig_ref[update : update + 1, :], (128, 128)).T
@@ -273,17 +292,35 @@
 
     def turn_right():
         for jb in range(8):
-            block = buffers[0]["all_first"][jb // 2, jb % 2].reshape(1024, 128).T.reshape(4, 2, 16, 1024)
             for half in range(2):
-                right_t[half, pl.ds(jb * 4, 4)] = block[:, half]
-
-    def contract_outgoing(half, yq):
+                block = buffers[0]["all_first"][jb // 2, jb % 2, :, :, half].reshape(512, 128).T
+                for k in range(2):
+                    piece = block[k * 64 : (k + 1) * 64].reshape(2, 2, 16, 512)
+                    cols = pl.ds(jb * 4 + half * 2, 2)
+                    for j_half in range(2):
+                        right_t[j_half, cols, :, pl.ds(k * 512, 512)] = piece[:, j_half]
+
+    def turn_left():
+        for kb in range(8):
+            parts = [buffers[1]["all_first"][kb // 2, kb % 2, :, :, half].reshape(512, 128) for half in range(2)]
+            for k, piece in enumerate(halves_of_lanes(*parts)):
+                left_n[kb, :, k] = piece.reshape(32, 16, 128)
+
+    def contract_outgoing(half):
         b = buffers[0]
-        rows = right_t[half].reshape(512, 1024)
-        operand = jnp.concatenate([b["all_last"][yq, k].reshape(1024, 128) for k in range(2)], axis=1)
-        product = jnp.dot(rows, operand, preferred_element_type=F32).astype(BF)
-        for k in range(2):
-            b["tri"][half, yq, k] = product[:, k * 128 : (k + 1) * 128].reshape(32, 16, 128)
+        columns = []
+        for yq in range(2):
+            parts = [b["all_last"][yq, k, :, half].reshape(512, 128) for k in range(2)]
+            columns.append(jnp.concatenate(halves_of_lanes(*parts), axis=0))
+        operand = jnp.concatenate(columns, axis=1)
+        products = [
+            jnp.dot(right_t[k].reshape(512, 1024), operand, preferred_element_type=F32).astype(BF)
+            for k in range(2)
+        ]
+        for yq in range(2):
+            parts = [product[:, yq * 128 : (yq + 1) * 128] for product in products]
+            for k, piece in enumerate(halves_of_lanes(*parts)):
+                b["tri"][half, yq, k] = piece.reshape(32, 16, 128)
 
     def contract_incoming(half):
         b = buffers[1]
@@ -291,7 +328,7 @@
         for part in range(4):
             operand = jnp.concatenate(
                 [
-                    b["all_first"][k // 2, k % 2, pl.ds(part * 4, 4)].reshape(256, 128)
+                    left_n[k, pl.ds(part * 8, 8)].reshape(256, 128)
                     for k in range(8)
                 ],
                 axis=1,
@@ -399,9 +436,8 @@
     scope("turn_right", turn_right)
     for half in range(2):
         arrived(0, f"last{half}")
-    for half in range(2):
+        scope("contract", contract_outgoing, half)
         for yq in range(2):
-            scope("contract", contract_outgoing, half, yq)
             scope("send_tri", send_rows, half, yq)
 
     b = buffers[1]
@@ -411,19 +447,22 @@
         scope("normalise", normalise, 1, state, half)
         scope("project", project, 1, 0, b["first"], half)
         scope("send_first", send_same_core, 1, f"first{half}", "first", b["first"], half)
-    for half in range(2):
+    scope("unfold", unfold)
+    for half in range(2):
+        scope("normalise", normalise, 1, start, half)
         scope("project", project, 1, 1, b["last"], half)
         scope("send_last", send_same_core, 1, f"last{half}", "last", b["last"], half)
     for half in range(2):
         scope("gates", gates, 1, half)
     exchange(1)
+    scope("turn_left", turn_left)
     for half in range(2):
         arrived(1, f"last{half}")
         scope("contract", contract_incoming, half)
         scope("send_tri", send_triangle, half)
     for half in range(2):
         arrived(1, f"tri{half}")
-        scope("finish", finish, 1, half, state)
+        scope("finish", finish, 1, half, start)
 
     for u in range(2):
         for name in FLOWS:
@@ -450,6 +489,7 @@
             pltpu.VMEM((128, 4096), BF),
             pltpu.VMEM((128 * PITCH, 128), F32),
             pltpu.VMEM((2, 32, 16, 1024), BF),
+            pltpu.VMEM((8, 32, 2, 16, 128), BF),
             pltpu.VMEM((256, 16, 128), BF),
             pltpu.SemaphoreType.DMA((2 * len(FLOWS),)),
             pltpu.SemaphoreType.DMA((2 * len(FLOWS),)),

time: 157 us -> 153 us (0.975)
  Pallas kernels: 155 us -> 152 us
    pallas_call x1, Pallas kernels: 155 us -> 152 us  [local(): pl.pallas_call(kernel, out_shape=jax.ShapeDtypeStruct((128, 32, 128), BF)...]
where the time goes in v4:
time: 153 us
  Pallas kernels  152 us (99%)
    pallas_call x1, Pallas kernels, local(): pl.pallas_call(kernel, out_shape=jax.ShapeDtypeStruct((128, 32, 128), BF)...  152 us

profile of v4, /device:TPU:1, one launch (start us, length us, event | category | flops | bytes accessed | tf_op | source)
XLA Modules:
  0.0 153.2 jit_solution(4419106515390313502)
XLA Ops:
  0.0 152.2 %shard_map.64 = bf16[128,32,128]{2,1,0:T(8,128)(2,1)S(1)} custom-call(bf16[128,32,128]{2,1,0:T(8,128)(2,1)} %x_in.1, bf16[2,4,128,128]{3,2,1,0:T(8,128)(2,1)} %pw_in.1, bf16[2,128,128]{2,1,0:T(8,128)(2,1)} %gw_in.1, bf16[2,128,128]{2,1,0:T(8,128)(2,1)} %ow_in.1, f32[2,128]{1,0:T(2,128)} %ig_in.1, f32[2,128]{1,0:T(2,128)} %og_in.1), custom_call_target="tpu_custom_call" | custom-call | tf_op jit(solution)/shard_map/pallas_call | solution.py:478
  152.2 1.0 copy.8

commit v5 on v4

--- a/solution.py
+++ b/solution.py
@@ -12,7 +12,8 @@
 PITCH = 40
 LANES = 512
 
-FLOWS = ("first0", "first1", "swap", "last0", "last1", "tri0", "tri1")
+FLOWS = ("first0", "first1", "swap", "last0", "last1", "tri0", "tri1", "pass0", "pass1")
+NEAR = ((3, 0), (5, 1), (2, 0), (6, 1), (1, 0), (7, 1))
 
 
 def scratch_of(update):
@@ -20,9 +21,9 @@
     return {
         "first": (128, 2) + tile,
         "last": (128, 2) + tile,
-        "all_first": (4, 2, 16, 2, 2) + tile,
-        "all_last": ((2, 2, 32, 2) if update == 0 else (8, 16, 2)) + tile,
-        "tri": ((2, 2, 2, 32) if update == 0 else (2, 8, 16)) + tile,
+        "all_first": ((4, 2, 16, 2, 2) if update == 0 else (2, 4, 2, 8, 2, 2, 2)) + tile,
+        "all_last": ((2, 2, 32, 2) if update == 0 else (2, 8, 4, 2, 2)) + tile,
+        "tri": ((2, 2, 2, 32) if update == 0 else (2, 2, 8, 4, 2)) + tile,
         "back": (2, 128) + tile,
     }
 
@@ -110,11 +111,13 @@
                 wait(tiles)
 
         if name == "swap":
-            wait(256)
-        elif update == 0 and not name.startswith("first"):
+            wait(256 * (update + 1))
+        elif update == 1:
+            wait(128 if name.startswith("pass") else 126)
+        elif name.startswith("first"):
+            wait(127)
+        else:
             wait_less(128, here_side, 1)
-        else:
-            wait(127)
 
     def arrived(update, name):
         with jax.named_scope(f"wait_{name}_{update}"):
@@ -134,20 +137,63 @@
             ty = lax.rem(y + far_first(lax.div(step, 4), 4), 4)
             one(tx, ty, z)
 
-    def send_same_core(update, name, which, source, half):
-        landing = buffers[update]["all_" + which]
-        if which == "first":
-            slot = landing.at[y, xl, chip_of_col, core, half]
-        else:
-            slot = landing.at[row, chip_of_col, half]
+    def send_right(name, source, half):
+        slot = buffers[0]["all_first"].at[y, xl, chip_of_col, core, half]
 
         def one(tx, ty, tz):
             copy(
-                update, name, source.at[tz * 16 + ty * 4 + tx, half], slot, device(tx, ty, tz, core)
+                0, name, source.at[tz * 16 + ty * 4 + tx, half], slot, device(tx, ty, tz, core)
             ).start()
 
         to_chips(one)
         slot[...] = source[channel, half]
+
+    def to_near(one):
+        @pl.loop(0, 16)
+        def _(step):
+            tx = lax.rem(x + far_first(lax.rem(step, 4), 4), 4)
+            ty = lax.rem(y + far_first(lax.div(step, 4), 4), 4)
+            for hops, role in NEAR:
+                one(tx, ty, hops, role)
+
+        @pl.loop(0, 15)
+        def _(step):
+            tx = lax.rem(x + far_first(lax.rem(step, 4), 4), 4)
+            ty = lax.rem(y + far_first(lax.div(step, 4), 4), 4)
+            for role in range(2):
+                one(tx, ty, 0, role)
+
+    def channel_at(tx, ty, tz, role):
+        return lax.rem(tz + 8 - role, 8) * 16 + ty * 4 + tx
+
+    def send_near(which, half):
+        b = buffers[1]
+
+        def slot(hops, role):
+            if which == "first":
+                return b["all_first"].at[role, y, xl, z, xh, core, half]
+            return b["all_last"].at[role, row, hops if role == 0 else (8 - hops) % 8, xh, half]
+
+        def one(tx, ty, hops, role):
+            tz = lax.rem(z + hops, 8)
+            copy(
+                1, f"{which}{half}", b[which].at[channel_at(tx, ty, tz, role), half],
+                slot(hops, role), device(tx, ty, tz, core),
+            ).start()
+
+        to_near(one)
+        for role in range(2):
+            slot(0, role)[...] = b[which][channel_at(x, y, z, role), half]
+
+    def pass_left(half):
+        whole = buffers[1]["all_first"]
+        for away in range(4):
+            for role in range(2):
+                came = lax.rem(z + (8 - away if role == 0 else away), 8)
+                to = device(x, y, lax.rem(z + (1 if role == 0 else 7), 8), core)
+                src = whole.at[role, :, :, came, :, core, half]
+                dst = whole.at[1 - role, :, :, came, :, core, half]
+                copy(1, f"pass{half}", src, dst, to).start()
 
     def send_left(name, source, half):
         slot = buffers[0]["all_last"].at[lax.rem(y, 2), xl, col, half]
@@ -200,14 +246,19 @@
 
     def send_triangle(half):
         b = buffers[1]
-        slot = b["back"].at[half, channel]
-
-        def one(tx, ty, tz):
-            src = b["tri"].at[half, ty * 2 + lax.rem(tx, 2), tz * 2 + lax.div(tx, 2)]
-            copy(1, f"tri{half}", src, slot, device(tx, ty, tz, core)).start()
-
-        to_chips(one)
-        slot[...] = b["tri"][half, row, chip_of_col]
+
+        def slot(role):
+            return b["back"].at[half, channel_at(x, y, z, role)]
+
+        def one(tx, ty, hops, role):
+            away = hops if role == 0 else (8 - hops) % 8
+            src = b["tri"].at[half, role, ty * 2 + lax.rem(tx, 2), away, lax.div(tx, 2)]
+            target = device(tx, ty, lax.rem(z + 8 - hops, 8), core)
+            copy(1, f"tri{half}", src, slot(role), target).start()
+
+        to_near(one)
+        for role in range(2):
+            slot(role)[...] = b["tri"][half, role, row, 0, xh]
 
     def turn_weight(update, index, weight):
         wt[update, index] = weight.astype(F32).T.astype(BF)
@@ -301,10 +352,12 @@
                         right_t[j_half, cols, :, pl.ds(k * 512, 512)] = piece[:, j_half]
 
     def turn_left():
-        for kb in range(8):
-            parts = [buffers[1]["all_first"][kb // 2, kb % 2, :, :, half].reshape(512, 128) for half in range(2)]
-            for k, piece in enumerate(halves_of_lanes(*parts)):
-                left_n[kb, :, k] = piece.reshape(32, 16, 128)
+        for role in range(2):
+            for kb in range(8):
+                whole = buffers[1]["all_first"]
+                parts = [whole[role, kb // 2, kb % 2, :, :, :, half].reshape(512, 128) for half in range(2)]
+                for k, piece in enumerate(halves_of_lanes(*parts)):
+                    left_n[role, kb, :, k] = piece.reshape(32, 16, 128)
 
     def contract_outgoing(half):
         b = buffers[0]
@@ -324,20 +377,20 @@
 
     def contract_incoming(half):
         b = buffers[1]
-        rows = jnp.concatenate([b["all_last"][k, :, half].reshape(256, 128) for k in range(8)], axis=1)
-        for part in range(4):
-            operand = jnp.concatenate(
-                [
-                    left_n[k, pl.ds(part * 8, 8)].reshape(256, 128)
-                    for k in range(8)
-                ],
-                axis=1,
+        for role in range(2):
+            rows = jnp.concatenate(
+                [b["all_last"][role, k, :, :, half].reshape(128, 128) for k in range(8)], axis=1
             )
-            product = lax.dot_general(
-                rows, operand, (((1,), (1,)), ((), ())), preferred_element_type=F32
-            ).astype(BF)
-            for k in range(2):
-                b["tri"][half, part * 2 + k] = product[:, k * 128 : (k + 1) * 128].reshape(16, 16, 128)
+            for part in range(4):
+                operand = jnp.concatenate(
+                    [left_n[role, k, pl.ds(part * 8, 8)].reshape(256, 128) for k in range(8)], axis=1
+                )
+                product = lax.dot_general(
+                    rows, operand, (((1,), (1,)), ((), ())), preferred_element_type=F32
+                ).astype(BF)
+                for k in range(2):
+                    piece = product[:, k * 128 : (k + 1) * 128].reshape(4, 2, 16, 128)
+                    b["tri"][half, role, part * 2 + k] = piece
 
     def finish(update, half, old):
         source = buffers[update]["back"]
@@ -410,7 +463,7 @@
         if half == 0:
             with jax.named_scope("barrier"):
                 pl.semaphore_wait(barrier, 255)
-        scope("send_first", send_same_core, 0, f"first{half}", "first", b["first"], half)
+        scope("send_first", send_right, f"first{half}", b["first"], half)
     for half in range(2):
         scope("project", project, 0, 0, b["last"], half)
         scope("send_last", send_left, f"last{half}", b["last"], half)
@@ -425,14 +478,15 @@
     for half in range(2):
         scope("gates", gates, 0, half)
 
-    def exchange(update):
-        for half in range(2):
-            arrived(update, f"first{half}")
-        own = buffers[update]["all_first"].at[:, :, :, core]
+    def swap(update):
+        whole = buffers[update]["all_first"]
+        own = whole.at[:, :, :, core] if update == 0 else whole.at[:, :, :, :, :, core]
         copy(update, "swap", own, own, device(x, y, z, other)).start()
         arrived(update, "swap")
 
-    exchange(0)
+    for half in range(2):
+        arrived(0, f"first{half}")
+    swap(0)
     scope("turn_right", turn_right)
     for half in range(2):
         arrived(0, f"last{half}")
@@ -446,15 +500,21 @@
         scope("finish", finish, 0, half, start)
         scope("normalise", normalise, 1, state, half)
         scope("project", project, 1, 0, b["first"], half)
-        scope("send_first", send_same_core, 1, f"first{half}", "first", b["first"], half)
+        scope("send_first", send_near, "first", half)
     scope("unfold", unfold)
     for half in range(2):
         scope("normalise", normalise, 1, start, half)
         scope("project", project, 1, 1, b["last"], half)
-        scope("send_last", send_same_core, 1, f"last{half}", "last", b["last"], half)
     for half in range(2):
         scope("gates", gates, 1, half)
-    exchange(1)
+    for half in range(2):
+        arrived(1, f"first{half}")
+        scope("pass", pass_left, half)
+    for half in range(2):
+        scope("send_last", send_near, "last", half)
+    for half in range(2):
+        arrived(1, f"pass{half}")
+    swap(1)
     scope("turn_left", turn_left)
     for half in range(2):
         arrived(1, f"last{half}")
@@ -466,7 +526,8 @@
 
     for u in range(2):
         for name in FLOWS:
-            waits(u, name, "send")
+            if u == 1 or not name.startswith("pass"):
+                waits(u, name, "send")
 
 
 def local(pair_rep, proj_weight, gate_weight, out_weight, in_gain, out_gain):
@@ -489,8 +550,8 @@
             pltpu.VMEM((128, 4096), BF),
             pltpu.VMEM((128 * PITCH, 128), F32),
             pltpu.VMEM((2, 32, 16, 1024), BF),
-            pltpu.VMEM((8, 32, 2, 16, 128), BF),
-            pltpu.VMEM((256, 16, 128), BF),
+            pltpu.VMEM((2, 8, 32, 2, 16, 128), BF),
+            pltpu.VMEM((512, 16, 128), BF),
             pltpu.SemaphoreType.DMA((2 * len(FLOWS),)),
             pltpu.SemaphoreType.DMA((2 * len(FLOWS),)),
             pltpu.VMEM((128, 32, 128), BF),
@@ -502,7 +563,7 @@
             pltpu.SemaphoreType.DMA((6,)),
         ],
         compiler_params=pltpu.CompilerParams(
-            collective_id=0, has_side_effects=True, vmem_limit_bytes=36 * 1024 * 1024
+            collective_id=0, has_side_effects=True, vmem_limit_bytes=44 * 1024 * 1024
         ),
     )(*inputs)
 

time: 153 us -> 148 us (0.967)
  Pallas kernels: 152 us -> 147 us
    pallas_call x1, Pallas kernels: 152 us -> 147 us  [local(): pl.pallas_call(kernel, out_shape=jax.ShapeDtypeStruct((128, 32, 128), BF)...]
where the time goes in v5:
time: 148 us
  Pallas kernels  147 us (99%)
    pallas_call x1, Pallas kernels, local(): pl.pallas_call(kernel, out_shape=jax.ShapeDtypeStruct((128, 32, 128), BF)...  147 us

profile of v5, /device:TPU:1, one launch (start us, length us, event | category | flops | bytes accessed | tf_op | source)
XLA Modules:
  0.0 148.0 jit_solution(17665767523829113801)
XLA Ops:
  0.0 147.0 %shard_map.64 = bf16[128,32,128]{2,1,0:T(8,128)(2,1)S(1)} custom-call(bf16[128,32,128]{2,1,0:T(8,128)(2,1)} %x_in.1, bf16[2,4,128,128]{3,2,1,0:T(8,128)(2,1)} %pw_in.1, bf16[2,128,128]{2,1,0:T(8,128)(2,1)} %gw_in.1, bf16[2,128,128]{2,1,0:T(8,128)(2,1)} %ow_in.1, f32[2,128]{1,0:T(2,128)} %ig_in.1, f32[2,128]{1,0:T(2,128)} %og_in.1), custom_call_target="tpu_custom_call" | custom-call | tf_op jit(solution)/shard_map/pallas_call | solution.py:539
  147.0 1.0 copy.8

commit v6 on v5

--- a/solution.py
+++ b/solution.py
@@ -244,21 +244,29 @@
         def _():
             one(x, z, core)
 
-    def send_triangle(half):
+    def send_triangle(half, step):
         b = buffers[1]
+        ty = lax.rem(y + far_first(step, 4), 4)
+        contract_incoming(half, ty)
 
         def slot(role):
             return b["back"].at[half, channel_at(x, y, z, role)]
 
-        def one(tx, ty, hops, role):
+        def one(tx, hops, role):
             away = hops if role == 0 else (8 - hops) % 8
             src = b["tri"].at[half, role, ty * 2 + lax.rem(tx, 2), away, lax.div(tx, 2)]
             target = device(tx, ty, lax.rem(z + 8 - hops, 8), core)
             copy(1, f"tri{half}", src, slot(role), target).start()
 
-        to_near(one)
-        for role in range(2):
-            slot(role)[...] = b["tri"][half, role, row, 0, xh]
+        for k in range(4):
+            for hops, role in NEAR:
+                one(lax.rem(x + far_first(k, 4), 4), hops, role)
+        for k in range(3 if step == 3 else 4):
+            for role in range(2):
+                one(lax.rem(x + far_first(k, 4), 4), 0, role)
+        if step == 3:
+            for role in range(2):
+                slot(role)[...] = b["tri"][half, role, row, 0, xh]
 
     def turn_weight(update, index, weight):
         wt[update, index] = weight.astype(F32).T.astype(BF)
@@ -375,22 +383,21 @@
             for k, piece in enumerate(halves_of_lanes(*parts)):
                 b["tri"][half, yq, k] = piece.reshape(32, 16, 128)
 
-    def contract_incoming(half):
+    def contract_incoming(half, part):
         b = buffers[1]
         for role in range(2):
             rows = jnp.concatenate(
                 [b["all_last"][role, k, :, :, half].reshape(128, 128) for k in range(8)], axis=1
             )
-            for part in range(4):
-                operand = jnp.concatenate(
-                    [left_n[role, k, pl.ds(part * 8, 8)].reshape(256, 128) for k in range(8)], axis=1
-                )
-                product = lax.dot_general(
-                    rows, operand, (((1,), (1,)), ((), ())), preferred_element_type=F32
-                ).astype(BF)
-                for k in range(2):
-                    piece = product[:, k * 128 : (k + 1) * 128].reshape(4, 2, 16, 128)
-                    b["tri"][half, role, part * 2 + k] = piece
+            operand = jnp.concatenate(
+                [left_n[role, k, pl.ds(part * 8, 8)].reshape(256, 128) for k in range(8)], axis=1
+            )
+            product = lax.dot_general(
+                rows, operand, (((1,), (1,)), ((), ())), preferred_element_type=F32
+            ).astype(BF)
+            for k in range(2):
+                piece = product[:, k * 128 : (k + 1) * 128].reshape(4, 2, 16, 128)
+                b["tri"][half, role, part * 2 + k] = piece
 
     def finish(update, half, old):
         source = buffers[update]["back"]
@@ -518,8 +525,8 @@
     scope("turn_left", turn_left)
     for half in range(2):
         arrived(1, f"last{half}")
-        scope("contract", contract_incoming, half)
-        scope("send_tri", send_triangle, half)
+        for step in range(4):
+            scope("send_tri", send_triangle, half, step)
     for half in range(2):
         arrived(1, f"tri{half}")
         scope("finish", finish, 1, half, start)

time: 148 us -> 148 us (level)
  no operation moved by 1% of the time
where the time goes in v6:
time: 148 us
  Pallas kernels  147 us (99%)
    pallas_call x1, Pallas kernels, local(): pl.pallas_call(kernel, out_shape=jax.ShapeDtypeStruct((128, 32, 128), BF)...  147 us

profile of v6, /device:TPU:1, one launch (start us, length us, event | category | flops | bytes accessed | tf_op | source)
XLA Modules:
  0.0 148.0 jit_solution(4804442226293098539)
XLA Ops:
  0.0 147.0 %shard_map.64 = bf16[128,32,128]{2,1,0:T(8,128)(2,1)S(1)} custom-call(bf16[128,32,128]{2,1,0:T(8,128)(2,1)} %x_in.1, bf16[2,4,128,128]{3,2,1,0:T(8,128)(2,1)} %pw_in.1, bf16[2,128,128]{2,1,0:T(8,128)(2,1)} %gw_in.1, bf16[2,128,128]{2,1,0:T(8,128)(2,1)} %ow_in.1, f32[2,128]{1,0:T(2,128)} %ig_in.1, f32[2,128]{1,0:T(2,128)} %og_in.1), custom_call_target="tpu_custom_call" | custom-call | tf_op jit(solution)/shard_map/pallas_call | solution.py:546
  147.0 1.0 copy.8
